TPU v7x, 32 devices: a whole 2x2x4 slice. The times are simulated.
32 devices in a mesh: dp: 8 (over y, x, core), expert: 4 (over z).
Axes of the slice: x: 2, y: 2, z: 4, core: 2. Of those that a mesh axis runs over, the one named last changes fastest.
Arguments:
- tokens: bfloat16 [4096, 2048], P(('dp', 'expert')), may hold values from -6 to 6
- out_grad: bfloat16 [4096, 2048], P(('dp', 'expert')), may hold values from -6 to 6
- gate_prob: float32 [4096, 1], P(('dp', 'expert')), may hold values from 0.2 to 1
- routing: int32 [4096, 1], P(('dp', 'expert')), may hold values from 0 to 3; in each aligned block of 128 rows (0 to 127, 128 to 255, ...) at most 64 rows name the same one
- expert_weights: bfloat16 [4, 2048, 1152], P('expert'), may hold values from -0.125 to 0.125
Outputs:
- input_grad: bfloat16 [4096, 2048], P(('dp', 'expert'))
- weight_grad: float32 [4, 2048, 1152], P('expert', 'dp')
Inputs may be any that keep to these rules, and one draw needn't show every extreme that they name: `routing`: among the tokens of one device at most 64 go to any one expert; in some devices' tokens an expert gets exactly 64.
All inputs are finite; a program needn't handle non-finite values.
Results may differ from a plain program's by a relative error of at most 0.014.
Values may be sent and summed in bfloat16 or wider, within the bound.
A program may use at most 64 MiB of HBM per device.

v0:
```python
import functools
import math
import jax
import jax.numpy as jnp
from jax import lax
from jax.experimental import pallas as pl
from jax.experimental.pallas import tpu as pltpu
from jax.sharding import PartitionSpec as P

MESH = pl.DeviceIdType.MESH
F32 = jnp.float32
BF16 = jnp.bfloat16
SUBS = 2
PIECES = 4


def xor(value, step):
    total, bit = 0, 1
    result = value
    while bit <= step:
        if step & bit:
            result = result + bit - 2 * bit * (lax.rem(lax.div(value, bit), 2))
        bit *= 2
    return result


def plan(n_expert, n_dp):
    half, quarter = n_expert // 2, n_expert // 4
    near = list(range(1, half))
    across = list(range(n_expert - 1, half + quarter - 1, -1))
    last = list(range(half + quarter - 1, half - 1, -1))
    chips = n_dp // 2
    side = math.isqrt(chips)
    while chips % side:
        side -= 1
    return near, across, last, chips // side, side


def body(
    n_expert,
    n_dp,
    cap,
    tokens_ref,
    out_grad_ref,
    gate_ref,
    route_ref,
    w_hbm,
    in_grad_ref,
    w_grad_ref,
    w_ref,
    send_x,
    send_g,
    recv_x,
    recv_g,
    ret,
    arrived,
    pair,
    hidden,
    part,
    recv_a,
    send_b,
    recv_b,
    send_c,
    recv_c,
    w_sem,
    dx_s,
    dx_r,
    dg_s,
    dg_r,
    rt_s,
    rt_r,
    a_s,
    a_r,
    b_s,
    b_r,
    c_s,
    c_r,
):
    near, across, last, na, nb = plan(n_expert, n_dp)
    far = across + last
    me = lax.axis_index("expert")
    dp = lax.axis_index("dp")
    tok, width = tokens_ref.shape
    hid = w_ref.shape[1] // 3
    slots = n_expert * cap
    quarter_rows = slots // 4
    share = width // n_dp
    sub = share // SUBS
    grad_scale = float(tok * n_dp) ** (-0.5)
    core = lax.rem(dp, 2)
    chip = lax.div(dp, 2)
    pos_hi, pos_lo = lax.div(chip, na), lax.rem(chip, na)
    if na == nb:
        a = jnp.where(core == 0, pos_lo, pos_hi)
        b = jnp.where(core == 0, pos_hi, pos_lo)
    else:
        a, b = pos_lo, pos_hi

    def chip_of(a_at, b_at):
        plain = b_at * na + a_at
        if na == nb:
            return jnp.where(core == 0, plain, a_at * na + b_at)
        return plain

    def dp_of(a_at, b_at):
        return chip_of(a_at, b_at) * 2 + core

    w_copy = pltpu.make_async_copy(w_hbm.at[0], w_ref, w_sem)
    w_copy.start()

    barrier = pltpu.get_barrier_semaphore()
    partner = dp + 1 - 2 * core
    greeted = 0
    for k in near + far:
        pl.semaphore_signal(barrier, inc=1, device_id={"expert": xor(me, k)}, device_id_type=MESH)
        greeted += 1
    pl.semaphore_signal(barrier, inc=1, device_id={"dp": partner}, device_id_type=MESH)
    greeted += 1
    for s in range(1, na):
        pl.semaphore_signal(
            barrier, inc=1, device_id={"dp": dp_of(lax.rem(a + s, na), b)}, device_id_type=MESH
        )
        greeted += 1
    for t in range(1, nb):
        pl.semaphore_signal(
            barrier, inc=1, device_id={"dp": dp_of(a, lax.rem(b + t, nb))}, device_id_type=MESH
        )
        greeted += 1

    row_i = lax.broadcasted_iota(jnp.int32, (tok, tok), 0)
    col_i = lax.broadcasted_iota(jnp.int32, (tok, tok), 1)

    def column(row):
        return jnp.sum(jnp.where(row_i == col_i, row, 0.0), axis=1, keepdims=True)

    route_row = route_ref[...].astype(F32)
    route_col = column(route_row)
    same = route_col == route_row
    pos_row = jnp.sum(jnp.where(same & (row_i < col_i), 1.0, 0.0), axis=0, keepdims=True)
    pos_col = jnp.sum(jnp.where(same & (col_i < row_i), 1.0, 0.0), axis=1, keepdims=True)
    slot_row = route_row * cap + pos_row
    slot_col = route_col * cap + pos_col
    slot_at = lax.broadcasted_iota(jnp.int32, (slots, tok), 0).astype(F32)
    table = jnp.where(slot_at == slot_row, 1.0, 0.0).astype(BF16)
    slot_of = lax.broadcasted_iota(jnp.int32, (tok, slots), 1).astype(F32)
    table_t = jnp.where(slot_of == slot_col, 1.0, 0.0).astype(BF16)

    send_x[...] = jnp.dot(table, tokens_ref[...], preferred_element_type=F32).astype(BF16)
    scaled = (column(gate_ref[...]) * out_grad_ref[...].astype(F32)).astype(BF16)
    send_g[...] = jnp.dot(table, scaled, preferred_element_type=F32).astype(BF16)

    def rows_of(index):
        return pl.ds(pl.multiple_of(index * cap, cap), cap)

    pl.semaphore_wait(barrier, greeted)

    def dispatch(k, src, dst, s_sem, r_sem):
        peer = xor(me, k)
        return pltpu.make_async_remote_copy(
            src_ref=src.at[rows_of(peer)],
            dst_ref=dst.at[rows_of(me)],
            send_sem=s_sem.at[k],
            recv_sem=r_sem.at[k],
            device_id={"expert": peer},
            device_id_type=MESH,
        )

    x_copies = {k: dispatch(k, send_x, recv_x, dx_s, dx_r) for k in near + far}
    g_copies = {k: dispatch(k, send_g, recv_g, dg_s, dg_r) for k in near + far}
    returns = {k: dispatch(k, ret, arrived, rt_s, rt_r) for k in near + far}
    for k in near + far:
        x_copies[k].start()
        g_copies[k].start()

    recv_x[rows_of(me)] = send_x[rows_of(me)]
    recv_g[rows_of(me)] = send_g[rows_of(me)]
    w_copy.wait()

    mine = lax.div(me, n_expert // 4)

    def forward(start, size):
        rows = pl.ds(pl.multiple_of(start, cap), size)
        x = recv_x[rows]
        pre_gate = jnp.dot(x, w_ref[:, :hid], preferred_element_type=F32)
        pre_up = jnp.dot(x, w_ref[:, hid : 2 * hid], preferred_element_type=F32)
        grad_hidden = jnp.dot(recv_g[rows], w_ref[:, 2 * hid :], preferred_element_type=F32)
        sig = jax.nn.sigmoid(pre_gate)
        active = pre_gate * sig
        hidden[rows] = (active * pre_up).astype(BF16)
        grad_gate = grad_hidden * pre_up * (sig * (1.0 + pre_gate * (1.0 - sig)))
        pair[rows, :hid] = grad_gate.astype(BF16)
        pair[rows, hid:] = (grad_hidden * active).astype(BF16)

    def backward(start, size):
        rows = pl.ds(pl.multiple_of(start, cap), size)
        tile = min(512, width)

        @pl.loop(0, width // tile)
        def _(j):
            at = pl.ds(pl.multiple_of(j * tile, tile), tile)
            ret[rows, at] = lax.dot_general(
                pair[rows],
                w_ref[at, : 2 * hid],
                (((1,), (1,)), ((), ())),
                preferred_element_type=F32,
            ).astype(BF16)

    near_half = (lax.div(mine, 2) * 2 * quarter_rows, 2 * quarter_rows)
    across_quarter = (xor(mine, 3) * quarter_rows, quarter_rows)
    last_quarter = (xor(mine, 2) * quarter_rows, quarter_rows)
    for k in near:
        x_copies[k].wait_recv()
        g_copies[k].wait_recv()
    forward(*near_half)
    backward(*near_half)
    for k in near:
        returns[k].start()
    arrived[rows_of(me)] = ret[rows_of(me)]
    for k in across:
        x_copies[k].wait_recv()
        g_copies[k].wait_recv()
    forward(*across_quarter)
    backward(*across_quarter)
    for k in last:
        x_copies[k].wait_recv()
        g_copies[k].wait_recv()
    for k in across:
        returns[k].start()
    forward(*last_quarter)

    def weight_rows(start, size):
        at = pl.ds(pl.multiple_of(start, size), size)
        contract = (((0,), (0,)), ((), ()))
        part[at, : 2 * hid] = (
            grad_scale
            * lax.dot_general(recv_x[:, at], pair[...], contract, preferred_element_type=F32)
        ).astype(BF16)
        part[at, 2 * hid :] = (
            grad_scale
            * lax.dot_general(recv_g[:, at], hidden[...], contract, preferred_element_type=F32)
        ).astype(BF16)

    def band(chip_at, core_at, g):
        return pl.ds(pl.multiple_of((chip_at * 2 + core_at) * share + g * sub, sub), sub)

    bands = [(s, t) for s in range(1, na) for t in list(range(1, nb)) + [0]]
    bands += [(0, t) for t in list(range(1, nb)) + [0]]
    items = [(s, t, g) for s, t in bands for g in range(SUBS)]

    def item_chip(s, t):
        return chip_of(lax.rem(a + s, na), lax.rem(b + t, nb))

    banded = share % 128 == 0
    if not banded:

        @pl.loop(0, width // 256)
        def _(j):
            weight_rows(j * 256, 256)

    def pair_copy(index, chip_at, g):
        rows = band(chip_at, 1 - core, g)
        return pltpu.make_async_remote_copy(
            src_ref=part.at[rows],
            dst_ref=recv_a.at[pl.ds(pl.multiple_of(chip_at * share + g * sub, sub), sub)],
            send_sem=a_s.at[index],
            recv_sem=a_r.at[index],
            device_id={"dp": partner},
            device_id_type=MESH,
        )

    def partner_chip(s, t):
        if na == nb:
            a_at, b_at = lax.rem(b + s, na), lax.rem(a + t, nb)
            return jnp.where(core == 1, b_at * na + a_at, a_at * na + b_at)
        return item_chip(s, t)

    a_copies = []
    for index, (s, t, g) in enumerate(items):
        chip_at = partner_chip(s, t)
        if banded and g == 0:
            weight_rows((chip_at * 2 + 1 - core) * share, share)
        copy = pair_copy(index, chip_at, g)
        copy.start()
        a_copies.append(copy)

    backward(*last_quarter)
    for k in last:
        returns[k].start()

    def pair_sum(index, s, t, g):
        chip_at = item_chip(s, t)
        a_copies[index].wait_recv()
        return (
            part[band(chip_at, core, g)].astype(F32)
            + recv_a[pl.ds(pl.multiple_of(chip_at * share + g * sub, sub), sub)].astype(F32)
        )

    if banded:
        for s, t in bands:
            weight_rows((item_chip(s, t) * 2 + core) * share, share)

    b_copies = {}
    for index, (s, t, g) in enumerate(items):
        if s == 0:
            continue
        at = ((s - 1) * nb + t) * SUBS + g
        send_b[at] = pair_sum(index, s, t, g).astype(BF16)
        copy = pltpu.make_async_remote_copy(
            src_ref=send_b.at[at],
            dst_ref=recv_b.at[at],
            send_sem=b_s.at[at],
            recv_sem=b_r.at[at],
            device_id={"dp": dp_of(lax.rem(a + s, na), b)},
            device_id_type=MESH,
        )
        copy.start()
        b_copies[s, t, g] = copy
    c_copies = {}
    for index, (s, t, g) in enumerate(items):
        if s > 0:
            continue
        total = pair_sum(index, s, t, g)
        for s_from in range(1, na):
            b_copies[s_from, t, g].wait_recv()
            total = total + recv_b[((s_from - 1) * nb + t) * SUBS + g].astype(F32)
        if t > 0:
            at = (t - 1) * SUBS + g
            send_c[at] = total.astype(BF16)
            copy = pltpu.make_async_remote_copy(
                src_ref=send_c.at[at],
                dst_ref=recv_c.at[at],
                send_sem=c_s.at[at],
                recv_sem=c_r.at[at],
                device_id={"dp": dp_of(a, lax.rem(b + t, nb))},
                device_id_type=MESH,
            )
            copy.start()
            c_copies[t, g] = copy
        else:
            w_grad_ref[0, pl.ds(g * sub, sub)] = total
    for t in range(1, nb):
        for g in range(SUBS):
            c_copies[t, g].wait_recv()
            w_grad_ref[0, pl.ds(g * sub, sub)] += recv_c[(t - 1) * SUBS + g].astype(F32)

    for k in near + far:
        returns[k].wait_recv()
    in_grad_ref[...] = jnp.dot(table_t, arrived[...], preferred_element_type=F32).astype(BF16)

    for k in near + far:
        x_copies[k].wait_send()
        g_copies[k].wait_send()
        returns[k].wait_send()
    for copy in a_copies + list(b_copies.values()) + list(c_copies.values()):
        copy.wait_send()


def local(n_expert, n_dp, tokens, out_grad, gate_prob, routing, expert_weights):
    tok, width = tokens.shape
    full = expert_weights.shape[2]
    hid = full // 3
    cap = max(16, 2 * tok // n_expert)
    slots = n_expert * cap
    share = width // n_dp
    _, _, _, na, nb = plan(n_expert, n_dp)
    sub = share // SUBS
    chips = na * nb
    n_b, n_c = max(1, (na - 1) * nb) * SUBS, max(1, nb - 1) * SUBS
    dma = pltpu.SemaphoreType.DMA
    vmem = pl.BlockSpec(memory_space=pltpu.VMEM)
    early = pl.pallas_call(
        functools.partial(body, n_expert, n_dp, cap),
        out_shape=(
            jax.ShapeDtypeStruct((tok, width), BF16),
            jax.ShapeDtypeStruct((1, share, full), F32),
        ),
        in_specs=[vmem] * 4 + [pl.BlockSpec(memory_space=pl.ANY)],
        out_specs=(vmem, vmem),
        scratch_shapes=[
            pltpu.VMEM((width, full), BF16),
            pltpu.VMEM((slots, width), BF16),
            pltpu.VMEM((slots, width), BF16),
            pltpu.VMEM((slots, width), BF16),
            pltpu.VMEM((slots, width), BF16),
            pltpu.VMEM((slots, width), BF16),
            pltpu.VMEM((slots, width), BF16),
            pltpu.VMEM((slots, 2 * hid), BF16),
            pltpu.VMEM((slots, hid), BF16),
            pltpu.VMEM((width, full), BF16),
            pltpu.VMEM((chips * share, full), BF16),
            pltpu.VMEM((n_b, sub, full), BF16),
            pltpu.VMEM((n_b, sub, full), BF16),
            pltpu.VMEM((n_c, sub, full), BF16),
            pltpu.VMEM((n_c, sub, full), BF16),
            dma,
            dma((n_expert,)),
            dma((n_expert,)),
            dma((n_expert,)),
            dma((n_expert,)),
            dma((n_expert,)),
            dma((n_expert,)),
            dma((chips * SUBS,)),
            dma((chips * SUBS,)),
            dma((n_b,)),
            dma((n_b,)),
            dma((n_c,)),
            dma((n_c,)),
        ],
        compiler_params=pltpu.CompilerParams(
            collective_id=0, has_side_effects=True, vmem_limit_bytes=60 * 1024 * 1024
        ),
        name="moe_backward",
    )(tokens, out_grad, gate_prob.reshape(1, tok), routing.reshape(1, tok), expert_weights)
    return pl.pallas_call(
        write_out,
        out_shape=(
            jax.ShapeDtypeStruct((tok, width), BF16),
            jax.ShapeDtypeStruct((1, share, full), F32),
        ),
        in_specs=[pl.BlockSpec(memory_space=pl.ANY)] * 2,
        out_specs=(pl.BlockSpec(memory_space=pl.ANY),) * 2,
        scratch_shapes=[
            pltpu.VMEM((tok, width), BF16),
            pltpu.VMEM((1, share, full), F32),
            dma((2 * PIECES,)),
            dma((2 * PIECES,)),
        ],
        name="write_out",
    )(*early)


def write_out(in_grad_ref, w_grad_ref, in_grad_out, w_grad_out, x_held, w_held, in_s, out_s):
    moves = []
    for p in range(PIECES):
        for src, mid, dst in (
            (in_grad_ref, x_held, in_grad_out),
            (w_grad_ref.at[0], w_held.at[0], w_grad_out.at[0]),
        ):
            rows = src.shape[0] // PIECES
            at = pl.ds(p * rows, rows)
            n = len(moves)
            moves.append(
                (
                    pltpu.make_async_copy(src.at[at], mid.at[at], in_s.at[n]),
                    pltpu.make_async_copy(mid.at[at], dst.at[at], out_s.at[n]),
                )
            )
    for take, _ in moves:
        take.start()
    for take, put in moves:
        take.wait()
        put.start()
    for _, put in moves:
        put.wait()


def solution(mesh):
    tokens_spec = P(("dp", "expert"), None)
    return jax.shard_map(
        functools.partial(local, mesh.shape["expert"], mesh.shape["dp"]),
        mesh=mesh,
        in_specs=(tokens_spec, tokens_spec, tokens_spec, tokens_spec, P("expert", None, None)),
        out_specs=(tokens_spec, P("expert", "dp", None)),
        check_vma=False,
    )
```

profile of v0, /device:TPU:0, one launch (start us, length us, event | category | flops | bytes accessed | tf_op | source)
XLA Modules:
  0.0 85.4 jit_solution(8406087684264835199)
XLA Ops:
  0.6 82.5 %moe_backward.1 = (bf16[128,2048]{1,0:T(8,128)(2,1)}, f32[1,256,1152]{2,1,0:T(8,128)}) custom-call(bf16[128,2048]{1,0:T(8,128)(2,1)} %tokens_ref.1, bf16[128,2048]{1,0:T(8,128)(2,1)} %out_grad_ref.1, f32[1,128]{1,0:T(1,128)} %bitcast.2, s32[1,128]{1,0:T(1,128)} %bitcast.3, bf16[1,2048,1152]{2,1,0:T(8,128)(2,1)} %w_hbm.1), custom_call_target="tpu_custom_call" | custom-call | tf_op jit(solution)/shard_map/moe_backward/pallas_call | solution.py:371
  83.1 2.3 %write_out.1 = (bf16[128,2048]{1,0:T(8,128)(2,1)}, f32[1,256,1152]{2,1,0:T(8,128)}) custom-call(bf16[128,2048]{1,0:T(8,128)(2,1)} %get-tuple-element.4.in_grad_ref, f32[1,256,1152]{2,1,0:T(8,128)} %get-tuple-element.5.w_grad_ref), custom_call_target="tpu_custom_call" | custom-call | tf_op jit(solution)/shard_map/write_out/pallas_call | solution.py:414
where the time goes:
time: 85.6 us; the launch traced here: 85.4 us
  Pallas kernels  84.8 us (99%)
    pallas_call x1, Pallas kernels, local(): pl.pallas_call(functools.partial(body, n_expert, n_dp, cap), out_shape=(j...  82.5 us
    pallas_call x1, Pallas kernels, local(): pl.pallas_call(write_out, out_shape=(jax.ShapeDtypeStruct((tok, width), B...  2.32 us

commit v1 on v0

--- a/solution.py
+++ b/solution.py
@@ -34,6 +34,10 @@
     while chips % side:
         side -= 1
     return near, across, last, chips // side, side
+
+
+def can_exchange(width, n_expert, n_dp):
+    return n_expert == 4 and (width // n_dp) % 128 == 0
 
 
 def body(
@@ -75,9 +79,22 @@
     b_r,
     c_s,
     c_r,
+    band_x=None,
+    band_g=None,
+    terms=None,
+    bx_s=None,
+    bx_r=None,
+    bg_s=None,
+    bg_r=None,
+    tm_s=None,
+    tm_r=None,
+    fw_s=None,
+    fw_r=None,
 ):
     near, across, last, na, nb = plan(n_expert, n_dp)
     far = across + last
+    order = [0] + near + far
+    place = {k: p for p, k in enumerate(order)}
     me = lax.axis_index("expert")
     dp = lax.axis_index("dp")
     tok, width = tokens_ref.shape
@@ -86,6 +103,8 @@
     quarter_rows = slots // 4
     share = width // n_dp
     sub = share // SUBS
+    exchange = can_exchange(width, n_expert, n_dp)
+    early_rows = 3 * quarter_rows if exchange else slots
     grad_scale = float(tok * n_dp) ** (-0.5)
     core = lax.rem(dp, 2)
     chip = lax.div(dp, 2)
@@ -114,17 +133,14 @@
     for k in near + far:
         pl.semaphore_signal(barrier, inc=1, device_id={"expert": xor(me, k)}, device_id_type=MESH)
         greeted += 1
-    pl.semaphore_signal(barrier, inc=1, device_id={"dp": partner}, device_id_type=MESH)
-    greeted += 1
-    for s in range(1, na):
-        pl.semaphore_signal(
-            barrier, inc=1, device_id={"dp": dp_of(lax.rem(a + s, na), b)}, device_id_type=MESH
-        )
-        greeted += 1
-    for t in range(1, nb):
-        pl.semaphore_signal(
-            barrier, inc=1, device_id={"dp": dp_of(a, lax.rem(b + t, nb))}, device_id_type=MESH
-        )
+    if exchange:
+        dp_peers = [lax.rem(dp + j, n_dp) for j in range(1, n_dp)]
+    else:
+        dp_peers = [partner]
+        dp_peers += [dp_of(lax.rem(a + s, na), b) for s in range(1, na)]
+        dp_peers += [dp_of(a, lax.rem(b + t, nb)) for t in range(1, nb)]
+    for peer in dp_peers:
+        pl.semaphore_signal(barrier, inc=1, device_id={"dp": peer}, device_id_type=MESH)
         greeted += 1
 
     row_i = lax.broadcasted_iota(jnp.int32, (tok, tok), 0)
@@ -133,7 +149,11 @@
     def column(row):
         return jnp.sum(jnp.where(row_i == col_i, row, 0.0), axis=1, keepdims=True)
 
-    route_row = route_ref[...].astype(F32)
+    offset = jnp.bitwise_xor(route_ref[...], me)
+    block = jnp.zeros_like(offset)
+    for p, k in enumerate(order):
+        block = jnp.where(offset == k, p, block)
+    route_row = block.astype(F32)
     route_col = column(route_row)
     same = route_col == route_row
     pos_row = jnp.sum(jnp.where(same & (row_i < col_i), 1.0, 0.0), axis=0, keepdims=True)
@@ -149,16 +169,16 @@
     scaled = (column(gate_ref[...]) * out_grad_ref[...].astype(F32)).astype(BF16)
     send_g[...] = jnp.dot(table, scaled, preferred_element_type=F32).astype(BF16)
 
-    def rows_of(index):
-        return pl.ds(pl.multiple_of(index * cap, cap), cap)
+    def rows_of(k):
+        return pl.ds(place[k] * cap, cap)
 
     pl.semaphore_wait(barrier, greeted)
 
     def dispatch(k, src, dst, s_sem, r_sem):
         peer = xor(me, k)
         return pltpu.make_async_remote_copy(
-            src_ref=src.at[rows_of(peer)],
-            dst_ref=dst.at[rows_of(me)],
+            src_ref=src.at[rows_of(k)],
+            dst_ref=dst.at[rows_of(k)],
             send_sem=s_sem.at[k],
             recv_sem=r_sem.at[k],
             device_id={"expert": peer},
@@ -172,14 +192,12 @@
         x_copies[k].start()
         g_copies[k].start()
 
-    recv_x[rows_of(me)] = send_x[rows_of(me)]
-    recv_g[rows_of(me)] = send_g[rows_of(me)]
+    recv_x[rows_of(0)] = send_x[rows_of(0)]
+    recv_g[rows_of(0)] = send_g[rows_of(0)]
     w_copy.wait()
 
-    mine = lax.div(me, n_expert // 4)
-
     def forward(start, size):
-        rows = pl.ds(pl.multiple_of(start, cap), size)
+        rows = pl.ds(start, size)
         x = recv_x[rows]
         pre_gate = jnp.dot(x, w_ref[:, :hid], preferred_element_type=F32)
         pre_up = jnp.dot(x, w_ref[:, hid : 2 * hid], preferred_element_type=F32)
@@ -192,7 +210,7 @@
         pair[rows, hid:] = (grad_hidden * active).astype(BF16)
 
     def backward(start, size):
-        rows = pl.ds(pl.multiple_of(start, cap), size)
+        rows = pl.ds(start, size)
         tile = min(512, width)
 
         @pl.loop(0, width // tile)
@@ -205,9 +223,77 @@
                 preferred_element_type=F32,
             ).astype(BF16)
 
-    near_half = (lax.div(mine, 2) * 2 * quarter_rows, 2 * quarter_rows)
-    across_quarter = (xor(mine, 3) * quarter_rows, quarter_rows)
-    last_quarter = (xor(mine, 2) * quarter_rows, quarter_rows)
+    near_half = (0, 2 * quarter_rows)
+    across_quarter = (2 * quarter_rows, quarter_rows)
+    last_quarter = (3 * quarter_rows, quarter_rows)
+    late = pl.ds(3 * quarter_rows, quarter_rows)
+
+    def rows_from(index):
+        return pl.ds(pl.multiple_of(index * quarter_rows, quarter_rows), quarter_rows)
+
+    def columns_of(index):
+        return pl.ds(pl.multiple_of(index * share, share), share)
+
+    def band_copy(j, src, dst, s_sem, r_sem):
+        peer = lax.rem(dp + j, n_dp)
+        return pltpu.make_async_remote_copy(
+            src_ref=src.at[late, columns_of(peer)],
+            dst_ref=dst.at[rows_from(dp)],
+            send_sem=s_sem.at[j],
+            recv_sem=r_sem.at[j],
+            device_id={"dp": peer},
+            device_id_type=MESH,
+        )
+
+    def term_copy(c):
+        return pltpu.make_async_remote_copy(
+            src_ref=terms.at[rows_from(dp)],
+            dst_ref=terms.at[rows_from(dp)],
+            send_sem=tm_s.at[c],
+            recv_sem=tm_r.at[c],
+            device_id={"dp": lax.rem(chip + c, n_dp // 2) * 2 + core},
+            device_id_type=MESH,
+        )
+
+    def forward_copy(c):
+        source = lax.rem(chip + n_dp // 2 - c, n_dp // 2) * 2 + core
+        return pltpu.make_async_remote_copy(
+            src_ref=terms.at[rows_from(source)],
+            dst_ref=terms.at[rows_from(source)],
+            send_sem=fw_s.at[c],
+            recv_sem=fw_r.at[c],
+            device_id={"dp": partner},
+            device_id_type=MESH,
+        )
+
+    def last_step():
+        for k in last:
+            x_copies[k].wait_recv()
+            g_copies[k].wait_recv()
+        if exchange:
+            for j in range(1, n_dp):
+                band_copy(j, recv_x, band_x, bx_s, bx_r).start()
+                band_copy(j, recv_g, band_g, bg_s, bg_r).start()
+        for k in across:
+            returns[k].start()
+        forward(*last_quarter)
+        if exchange:
+            terms[rows_from(dp), : 2 * hid] = pair[late]
+            terms[rows_from(dp), 2 * hid :] = hidden[late]
+            for c in range(1, n_dp // 2):
+                term_copy(c).start()
+            forward_copy(0).start()
+            band_x[rows_from(dp)] = recv_x[late, columns_of(dp)]
+            band_g[rows_from(dp)] = recv_g[late, columns_of(dp)]
+            backward(*last_quarter)
+            for k in last:
+                returns[k].start()
+
+    def forward_terms():
+        for c in range(1, n_dp // 2):
+            term_copy(c).wait_recv()
+            forward_copy(c).start()
+
     for k in near:
         x_copies[k].wait_recv()
         g_copies[k].wait_recv()
@@ -215,29 +301,32 @@
     backward(*near_half)
     for k in near:
         returns[k].start()
-    arrived[rows_of(me)] = ret[rows_of(me)]
+    arrived[rows_of(0)] = ret[rows_of(0)]
     for k in across:
         x_copies[k].wait_recv()
         g_copies[k].wait_recv()
     forward(*across_quarter)
     backward(*across_quarter)
-    for k in last:
-        x_copies[k].wait_recv()
-        g_copies[k].wait_recv()
-    for k in across:
-        returns[k].start()
-    forward(*last_quarter)
+    if exchange:
+        first = (me > 0) & (me < n_expert - 1)
+        pl.when(first)(last_step)
+    else:
+        last_step()
 
     def weight_rows(start, size):
         at = pl.ds(pl.multiple_of(start, size), size)
         contract = (((0,), (0,)), ((), ()))
         part[at, : 2 * hid] = (
             grad_scale
-            * lax.dot_general(recv_x[:, at], pair[...], contract, preferred_element_type=F32)
+            * lax.dot_general(
+                recv_x[:early_rows, at], pair[:early_rows], contract, preferred_element_type=F32
+            )
         ).astype(BF16)
         part[at, 2 * hid :] = (
             grad_scale
-            * lax.dot_general(recv_g[:, at], hidden[...], contract, preferred_element_type=F32)
+            * lax.dot_general(
+                recv_g[:early_rows, at], hidden[:early_rows], contract, preferred_element_type=F32
+            )
         ).astype(BF16)
 
     def band(chip_at, core_at, g):
@@ -283,9 +372,10 @@
         copy.start()
         a_copies.append(copy)
 
-    backward(*last_quarter)
-    for k in last:
-        returns[k].start()
+    if not exchange:
+        backward(*last_quarter)
+        for k in last:
+            returns[k].start()
 
     def pair_sum(index, s, t, g):
         chip_at = item_chip(s, t)
@@ -315,6 +405,8 @@
         )
         copy.start()
         b_copies[s, t, g] = copy
+    if exchange:
+        pl.when(first)(forward_terms)
     c_copies = {}
     for index, (s, t, g) in enumerate(items):
         if s > 0:
@@ -343,6 +435,26 @@
             c_copies[t, g].wait_recv()
             w_grad_ref[0, pl.ds(g * sub, sub)] += recv_c[(t - 1) * SUBS + g].astype(F32)
 
+    if exchange:
+
+        @pl.when(jnp.logical_not(first))
+        def _():
+            last_step()
+            forward_terms()
+
+        for j in range(1, n_dp):
+            band_copy(j, recv_x, band_x, bx_s, bx_r).wait_recv()
+            band_copy(j, recv_g, band_g, bg_s, bg_r).wait_recv()
+        for c in range(n_dp // 2):
+            forward_copy(c).wait_recv()
+        contract = (((0,), (0,)), ((), ()))
+        w_grad_ref[0, :, : 2 * hid] += grad_scale * lax.dot_general(
+            band_x[...], terms[:, : 2 * hid], contract, preferred_element_type=F32
+        )
+        w_grad_ref[0, :, 2 * hid :] += grad_scale * lax.dot_general(
+            band_g[...], terms[:, 2 * hid :], contract, preferred_element_type=F32
+        )
+
     for k in near + far:
         returns[k].wait_recv()
     in_grad_ref[...] = jnp.dot(table_t, arrived[...], preferred_element_type=F32).astype(BF16)
@@ -351,6 +463,14 @@
         x_copies[k].wait_send()
         g_copies[k].wait_send()
         returns[k].wait_send()
+    if exchange:
+        for j in range(1, n_dp):
+            band_copy(j, recv_x, band_x, bx_s, bx_r).wait_send()
+            band_copy(j, recv_g, band_g, bg_s, bg_r).wait_send()
+        for c in range(n_dp // 2):
+            if c > 0:
+                term_copy(c).wait_send()
+            forward_copy(c).wait_send()
     for copy in a_copies + list(b_copies.values()) + list(c_copies.values()):
         copy.wait_send()
 
@@ -368,6 +488,15 @@
     n_b, n_c = max(1, (na - 1) * nb) * SUBS, max(1, nb - 1) * SUBS
     dma = pltpu.SemaphoreType.DMA
     vmem = pl.BlockSpec(memory_space=pltpu.VMEM)
+    extra = []
+    if can_exchange(width, n_expert, n_dp):
+        rows = n_dp * slots // 4
+        extra = [
+            pltpu.VMEM((rows, share), BF16),
+            pltpu.VMEM((rows, share), BF16),
+            pltpu.VMEM((rows, full), BF16),
+        ]
+        extra += [dma((n_dp,))] * 4 + [dma((chips,))] * 4
     early = pl.pallas_call(
         functools.partial(body, n_expert, n_dp, cap),
         out_shape=(
@@ -405,7 +534,8 @@
             dma((n_b,)),
             dma((n_c,)),
             dma((n_c,)),
-        ],
+        ]
+        + extra,
         compiler_params=pltpu.CompilerParams(
             collective_id=0, has_side_effects=True, vmem_limit_bytes=60 * 1024 * 1024
         ),

time: 85.6 us -> 81.8 us (0.956)
  Pallas kernels: 84.8 us -> 80.9 us
    pallas_call x1, Pallas kernels: 82.5 us -> 78.6 us  [local(): pl.pallas_call(functools.partial(body, n_expert, n_dp, cap), out_shape=(j...]
where the time goes in v1:
time: 81.8 us; the launch traced here: 81.6 us
  Pallas kernels  80.9 us (99%)
    pallas_call x1, Pallas kernels, local(): pl.pallas_call(functools.partial(body, n_expert, n_dp, cap), out_shape=(j...  78.6 us
    pallas_call x1, Pallas kernels, local(): pl.pallas_call(write_out, out_shape=(jax.ShapeDtypeStruct((tok, width), B...  2.32 us

profile of v1, /device:TPU:0, one launch (start us, length us, event | category | flops | bytes accessed | tf_op | source)
XLA Modules:
  0.0 81.6 jit_solution(13097410823388797492)
XLA Ops:
  0.6 78.6 %moe_backward.1 = (bf16[128,2048]{1,0:T(8,128)(2,1)}, f32[1,256,1152]{2,1,0:T(8,128)}) custom-call(bf16[128,2048]{1,0:T(8,128)(2,1)} %tokens_ref.1, bf16[128,2048]{1,0:T(8,128)(2,1)} %out_grad_ref.1, f32[1,128]{1,0:T(1,128)} %bitcast.2, s32[1,128]{1,0:T(1,128)} %bitcast.3, bf16[1,2048,1152]{2,1,0:T(8,128)(2,1)} %w_hbm.1), custom_call_target="tpu_custom_call" | custom-call | tf_op jit(solution)/shard_map/moe_backward/pallas_call | solution.py:500
  79.3 2.3 %write_out.1 = (bf16[128,2048]{1,0:T(8,128)(2,1)}, f32[1,256,1152]{2,1,0:T(8,128)}) custom-call(bf16[128,2048]{1,0:T(8,128)(2,1)} %get-tuple-element.4.in_grad_ref, f32[1,256,1152]{2,1,0:T(8,128)} %get-tuple-element.5.w_grad_ref), custom_call_target="tpu_custom_call" | custom-call | tf_op jit(solution)/shard_map/write_out/pallas_call | solution.py:544

commit v2 on v0

--- a/solution.py
+++ b/solution.py
@@ -355,6 +355,627 @@
         copy.wait_send()
 
 
+def paired(width, hid, n_expert, n_dp):
+    chips_a, chips_b = plan(n_expert, n_dp)[3:]
+    return n_expert == 4 and chips_a == chips_b == 2 and width % (128 * n_dp) == hid % 128 == 0
+
+
+def paired_body(
+    n_expert,
+    n_dp,
+    cap,
+    tokens_ref,
+    out_grad_ref,
+    gate_ref,
+    route_ref,
+    w_hbm,
+    in_grad_ref,
+    w_grad_ref,
+    w_ref,
+    w2_ref,
+    send_x,
+    send_g,
+    recv_x,
+    recv_g,
+    ret,
+    arrived,
+    pair,
+    hidden,
+    part,
+    recv_a,
+    send_b,
+    recv_b,
+    send_c,
+    recv_c,
+    stage,
+    band_x,
+    band_g,
+    terms,
+    held_d,
+    send_d,
+    near_d,
+    far_d,
+    w_sem,
+    st_sem,
+    dx_s,
+    dx_r,
+    dg_s,
+    dg_r,
+    rt_s,
+    rt_r,
+    a_s,
+    a_r,
+    b_s,
+    b_r,
+    c_s,
+    c_r,
+    bx_s,
+    bx_r,
+    bg_s,
+    bg_r,
+    tm_s,
+    tm_r,
+    fw_s,
+    fw_r,
+    w_s,
+    w_r,
+    wz_s,
+    ag_s,
+    ag_r,
+    pf_s,
+    pf_r,
+    d_s,
+    d_r,
+    f_r,
+):
+    _, _, _, na, nb = plan(n_expert, n_dp)
+    chips = na * nb
+    me = lax.axis_index("expert")
+    dp = lax.axis_index("dp")
+    half = lax.div(me, 2)
+    inner = (me == 1) | (me == n_expert - 2)
+    outer = jnp.logical_not(inner)
+    near = me + 1 - 2 * lax.rem(me, 2)
+    mirror = n_expert - 1 - me
+    inner_far = 2 - half
+    outer_far = 3 - 3 * half
+    tok, width = tokens_ref.shape
+    hid = w_ref.shape[1] // 3
+    slots = n_expert * cap
+    share = width // n_dp
+    sub = share // SUBS
+    grad_scale = float(tok * n_dp) ** (-0.5)
+    core = lax.rem(dp, 2)
+    chip = lax.div(dp, 2)
+    partner = dp + 1 - 2 * core
+    pos_hi, pos_lo = lax.div(chip, na), lax.rem(chip, na)
+    if na == nb:
+        a = jnp.where(core == 0, pos_lo, pos_hi)
+        b = jnp.where(core == 0, pos_hi, pos_lo)
+    else:
+        a, b = pos_lo, pos_hi
+
+    def chip_of(a_at, b_at):
+        plain = b_at * na + a_at
+        if na == nb:
+            return jnp.where(core == 0, plain, a_at * na + b_at)
+        return plain
+
+    def dp_of(a_at, b_at):
+        return chip_of(a_at, b_at) * 2 + core
+
+    def columns_of(index):
+        return pl.ds(pl.multiple_of(index * share, share), share)
+
+    w_copy = pltpu.make_async_copy(w_hbm.at[0], w_ref, w_sem)
+    slices = w2_ref.shape[0]
+    unit = hid // slices
+
+    def stage_copy(q, third):
+        return pltpu.make_async_copy(
+            w_hbm.at[0, columns_of(dp), pl.ds(third * hid + q * unit, unit)],
+            stage.at[q, :, pl.ds(third * unit, unit)],
+            st_sem.at[q * 3 + third],
+        )
+
+    @pl.when(outer)
+    def _():
+        for q in range(slices):
+            for third in range(3):
+                stage_copy(q, third).start()
+
+    w_copy.start()
+
+    barrier = pltpu.get_barrier_semaphore()
+    for k in range(1, n_expert):
+        peer = lax.rem(me + k, n_expert)
+        pl.semaphore_signal(barrier, inc=1, device_id={"expert": peer}, device_id_type=MESH)
+    for j in range(1, n_dp):
+        peer = lax.rem(dp + j, n_dp)
+        pl.semaphore_signal(barrier, inc=1, device_id={"dp": peer}, device_id_type=MESH)
+
+    row_i = lax.broadcasted_iota(jnp.int32, (tok, tok), 0)
+    col_i = lax.broadcasted_iota(jnp.int32, (tok, tok), 1)
+
+    def column(row):
+        return jnp.sum(jnp.where(row_i == col_i, row, 0.0), axis=1, keepdims=True)
+
+    route = route_ref[...]
+    block = jnp.where(route == near, 1, jnp.where(route == inner_far, 2, 3))
+    route_row = jnp.where(route == me, 0, block).astype(F32)
+    route_col = column(route_row)
+    same = route_col == route_row
+    pos_row = jnp.sum(jnp.where(same & (row_i < col_i), 1.0, 0.0), axis=0, keepdims=True)
+    pos_col = jnp.sum(jnp.where(same & (col_i < row_i), 1.0, 0.0), axis=1, keepdims=True)
+    slot_row = route_row * cap + pos_row
+    slot_col = route_col * cap + pos_col
+    slot_at = lax.broadcasted_iota(jnp.int32, (slots, tok), 0).astype(F32)
+    table = jnp.where(slot_at == slot_row, 1.0, 0.0).astype(BF16)
+    slot_of = lax.broadcasted_iota(jnp.int32, (tok, slots), 1).astype(F32)
+    table_t = jnp.where(slot_of == slot_col, 1.0, 0.0).astype(BF16)
+
+    send_x[...] = jnp.dot(table, tokens_ref[...], preferred_element_type=F32).astype(BF16)
+    scaled = (column(gate_ref[...]) * out_grad_ref[...].astype(F32)).astype(BF16)
+    send_g[...] = jnp.dot(table, scaled, preferred_element_type=F32).astype(BF16)
+
+    def rows_of(index):
+        return pl.ds(index * cap, cap)
+
+    kept = rows_of(3)
+
+    def rows_from(index):
+        return pl.ds(pl.multiple_of(index * cap, cap), cap)
+
+    def remote(src, dst, s_sem, r_sem, device):
+        return pltpu.make_async_remote_copy(
+            src_ref=src,
+            dst_ref=dst,
+            send_sem=s_sem,
+            recv_sem=r_sem,
+            device_id=device,
+            device_id_type=MESH,
+        )
+
+    pl.semaphore_wait(barrier, n_expert - 1 + n_dp - 1)
+
+    cross_at = jnp.where(inner, 2, 3)
+
+    def near_copy(src, dst, s_sem, r_sem):
+        return remote(
+            src.at[rows_of(1)], dst.at[rows_of(1)], s_sem.at[1], r_sem.at[1], {"expert": near}
+        )
+
+    def cross_copy(src, dst, s_sem, r_sem):
+        return remote(
+            src.at[rows_of(2)],
+            dst.at[rows_from(cross_at)],
+            s_sem.at[2],
+            r_sem.at[cross_at],
+            {"expert": inner_far},
+        )
+
+    def cross_arrival(index, dst, s_sem, r_sem):
+        return remote(
+            dst.at[rows_of(index)],
+            dst.at[rows_of(index)],
+            s_sem.at[2],
+            r_sem.at[index],
+            {"expert": mirror},
+        )
+
+    x_args = (send_x, recv_x, dx_s, dx_r)
+    g_args = (send_g, recv_g, dg_s, dg_r)
+
+    def return_copy(index):
+        peer = {1: near, 2: mirror, 3: outer_far}[index]
+        home = rows_of(min(index, 2))
+        return remote(
+            ret.at[rows_of(index)],
+            arrived.at[home],
+            rt_s.at[index],
+            rt_r.at[min(index, 2)],
+            {"expert": peer},
+        )
+
+    first = jnp.where(core == 0, 1, 2)
+
+    def beside(c):
+        return xor(chip, c)
+
+    chip_first = jnp.where(core == 0, beside(1), beside(2))
+    chip_second = jnp.where(core == 0, beside(2), beside(1))
+
+    def weight_out(q):
+        dst = w2_ref.at[q, columns_of(dp)]
+        return remote(stage.at[q], dst, w_s.at[q], w_r.at[q], {"expert": inner_far})
+
+    def weight_on(q):
+        at = w2_ref.at[q, columns_of(dp)]
+        return remote(at, at, wz_s.at[q], w_r.at[q], {"expert": near})
+
+    def spread(c, q):
+        at = w2_ref.at[q, columns_of(dp)]
+        n = c * slices + q
+        return remote(at, at, ag_s.at[n], ag_r.at[n], {"dp": beside(c) * 2 + core})
+
+    def relay(q):
+        at = w2_ref.at[q, columns_of(chip_first * 2 + core)]
+        n = 3 * slices + q
+        return remote(at, at, ag_s.at[n], ag_r.at[n], {"dp": chip_second * 2 + core})
+
+    def hand_over(c, q):
+        at = w2_ref.at[q, columns_of(beside(c) * 2 + core)]
+        n = c * slices + q
+        return remote(at, at, pf_s.at[n], pf_r.at[n], {"dp": partner})
+
+    def band_copy(j, src, dst, s_sem, r_sem):
+        peer = lax.rem(dp + j, n_dp)
+        return remote(
+            src.at[kept, columns_of(peer)],
+            dst.at[rows_from(dp)],
+            s_sem.at[j],
+            r_sem.at[j],
+            {"dp": peer},
+        )
+
+    bx_args = (send_x, band_x, bx_s, bx_r)
+    bg_args = (send_g, band_g, bg_s, bg_r)
+
+    def term_copy(c, q):
+        at = terms.at[q, rows_from(dp)]
+        n = c * slices + q
+        return remote(at, at, tm_s.at[n], tm_r.at[n], {"dp": beside(c) * 2 + core})
+
+    def term_over(c, q):
+        at = terms.at[q, rows_from(beside(c) * 2 + core)]
+        n = c * slices + q
+        return remote(at, at, fw_s.at[n], fw_r.at[n], {"dp": partner})
+
+    @pl.when(outer)
+    def _():
+        for q in range(slices):
+            for third in range(3):
+                stage_copy(q, third).wait()
+            weight_out(q).start()
+
+    near_copy(*x_args).start()
+    pl.when(outer)(lambda: near_copy(*g_args).start())
+    cross_copy(*x_args).start()
+    cross_copy(*g_args).start()
+    for j in range(1, n_dp):
+        band_copy(j, *bx_args).start()
+        band_copy(j, *bg_args).start()
+
+    recv_x[rows_of(0)] = send_x[rows_of(0)]
+    recv_g[rows_of(0)] = send_g[rows_of(0)]
+    band_x[rows_from(dp)] = send_x[kept, columns_of(dp)]
+    band_g[rows_from(dp)] = send_g[kept, columns_of(dp)]
+
+    @pl.when(outer)
+    def _():
+        rest = pl.ds(2 * cap, 2 * cap)
+        recv_x[rest] = jnp.zeros((2 * cap, width), BF16)
+        recv_g[rest] = jnp.zeros((2 * cap, width), BF16)
+        pair[rest] = jnp.zeros((2 * cap, 2 * hid), BF16)
+        hidden[rest] = jnp.zeros((2 * cap, hid), BF16)
+
+    def forward(x, g, weights):
+        third = weights.shape[1] // 3
+        pre_gate = jnp.dot(x, weights[:, :third], preferred_element_type=F32)
+        pre_up = jnp.dot(x, weights[:, third : 2 * third], preferred_element_type=F32)
+        grad_hidden = jnp.dot(g, weights[:, 2 * third :], preferred_element_type=F32)
+        sig = jax.nn.sigmoid(pre_gate)
+        active = pre_gate * sig
+        grad_gate = grad_hidden * pre_up * (sig * (1.0 + pre_gate * (1.0 - sig)))
+        return (
+            grad_gate.astype(BF16),
+            (grad_hidden * active).astype(BF16),
+            (active * pre_up).astype(BF16),
+        )
+
+    def forward_rows(start, size):
+        rows = pl.ds(start, size)
+        grad_gate, grad_up, kept_hidden = forward(recv_x[rows], recv_g[rows], w_ref)
+        pair[rows, :hid] = grad_gate
+        pair[rows, hid:] = grad_up
+        hidden[rows] = kept_hidden
+
+    def columns(pieces, dst, rows):
+        tile = min(512, width)
+
+        @pl.loop(0, width // tile)
+        def _(j):
+            at = pl.ds(pl.multiple_of(j * tile, tile), tile)
+            total = 0.0
+            for grads, weights in pieces:
+                total = total + lax.dot_general(
+                    grads(), weights(at), (((1,), (1,)), ((), ())), preferred_element_type=F32
+                )
+            dst[rows, at] = total.astype(BF16)
+
+    def backward_rows(start, size):
+        rows = pl.ds(start, size)
+        columns([(lambda: pair[rows], lambda at: w_ref[at, : 2 * hid])], ret, rows)
+
+    contract = (((0,), (0,)), ((), ()))
+    mine = rows_from(dp)
+
+    def kept_forward(q):
+        grad_gate, grad_up, kept_hidden = forward(send_x[kept], send_g[kept], w2_ref.at[q])
+        terms[q, mine, :unit] = grad_gate
+        terms[q, mine, unit : 2 * unit] = grad_up
+        terms[q, mine, 2 * unit :] = kept_hidden
+
+    def kept_grad(q):
+        first = lax.dot_general(
+            band_x[...], terms[q, :, : 2 * unit], contract, preferred_element_type=F32
+        )
+        second = lax.dot_general(
+            band_g[...], terms[q, :, 2 * unit :], contract, preferred_element_type=F32
+        )
+        return grad_scale * jnp.concatenate([first, second], axis=1)
+
+    def near_hop(q):
+        return remote(send_d.at[q], near_d.at[q], d_s.at[q], d_r.at[q], {"expert": near})
+
+    def far_hop(q):
+        return remote(send_d.at[q], far_d.at[q], d_s.at[q], f_r.at[q], {"expert": outer_far})
+
+    def take(q):
+        weight_on(q).wait_recv()
+        pl.when(inner)(lambda: weight_on(q).start())
+        for c in (1, 2):
+            spread(c, q).start()
+        hand_over(0, q).start()
+
+    def pass_on(q):
+        for c in (1, 2):
+            spread(c, q).wait_recv()
+        relay(q).start()
+        for c in (1, 2):
+            hand_over(c, q).start()
+
+    def pass_last(q):
+        relay(q).wait_recv()
+        hand_over(3, q).start()
+
+    def kept_terms(q):
+        for c in range(4):
+            hand_over(c, q).wait_recv()
+        kept_forward(q)
+        for c in range(1, 4):
+            term_copy(c, q).start()
+        term_over(0, q).start()
+
+    def pass_terms(q):
+        for c in range(1, 4):
+            term_copy(c, q).wait_recv()
+            term_over(c, q).start()
+
+    def kept_band(q):
+        if q == 0:
+            for j in range(1, n_dp):
+                band_copy(j, *bx_args).wait_recv()
+                band_copy(j, *bg_args).wait_recv()
+        for c in range(4):
+            term_over(c, q).wait_recv()
+        held_d[q] = kept_grad(q)
+
+        @pl.when(outer)
+        def _():
+            send_d[q] = held_d[q].astype(BF16)
+            near_hop(q).start()
+
+    def near_rows():
+        near_copy(*x_args).wait_recv()
+        near_copy(*g_args).wait_recv()
+        forward_rows(0, 2 * cap)
+        backward_rows(0, 2 * cap)
+        return_copy(1).start()
+        arrived[rows_of(0)] = ret[rows_of(0)]
+
+        @pl.when(inner)
+        def _():
+            cross_arrival(2, *x_args[1:]).wait_recv()
+            cross_arrival(2, *g_args[1:]).wait_recv()
+            forward_rows(2 * cap, cap)
+            backward_rows(2 * cap, cap)
+            return_copy(2).start()
+
+    def late_near():
+        @pl.when(inner)
+        def _():
+            near_copy(*g_args).start()
+            w_copy.wait()
+
+        pl.when(outer)(w_copy.wait)
+
+    take(0)
+    take(1)
+    pass_on(0)
+    take(2)
+    late_near()
+    pass_on(1)
+    pass_last(0)
+    kept_terms(0)
+    pass_on(2)
+    pass_last(1)
+    kept_terms(1)
+    pass_terms(0)
+    pass_last(2)
+    kept_terms(2)
+    kept_band(0)
+    pass_terms(1)
+    near_rows()
+    kept_band(1)
+    pass_terms(2)
+    kept_pieces = [
+        (lambda q=q: terms[q, mine, : 2 * unit], lambda at, q=q: w2_ref[q, at, : 2 * unit])
+        for q in range(slices)
+    ]
+    columns(kept_pieces, arrived, kept)
+    kept_band(2)
+
+    @pl.when(inner)
+    def _():
+        cross_arrival(3, *x_args[1:]).wait_recv()
+        cross_arrival(3, *g_args[1:]).wait_recv()
+        forward_rows(3 * cap, cap)
+
+    def weight_rows(start, size):
+        at = pl.ds(pl.multiple_of(start, size), size)
+        part[at, : 2 * hid] = (
+            grad_scale
+            * lax.dot_general(recv_x[:, at], pair[...], contract, preferred_element_type=F32)
+        ).astype(BF16)
+        part[at, 2 * hid :] = (
+            grad_scale
+            * lax.dot_general(recv_g[:, at], hidden[...], contract, preferred_element_type=F32)
+        ).astype(BF16)
+
+    def band(chip_at, core_at, g):
+        return pl.ds(pl.multiple_of((chip_at * 2 + core_at) * share + g * sub, sub), sub)
+
+    bands = [(s, t) for s in range(1, na) for t in list(range(1, nb)) + [0]]
+    bands += [(0, t) for t in list(range(1, nb)) + [0]]
+    items = [(s, t, g) for s, t in bands for g in range(SUBS)]
+
+    def item_chip(s, t):
+        return chip_of(lax.rem(a + s, na), lax.rem(b + t, nb))
+
+    def pair_copy(index, chip_at, g):
+        return remote(
+            part.at[band(chip_at, 1 - core, g)],
+            recv_a.at[pl.ds(pl.multiple_of(chip_at * share + g * sub, sub), sub)],
+            a_s.at[index],
+            a_r.at[index],
+            {"dp": partner},
+        )
+
+    def partner_chip(s, t):
+        if na == nb:
+            a_at, b_at = lax.rem(b + s, na), lax.rem(a + t, nb)
+            return jnp.where(core == 1, b_at * na + a_at, a_at * na + b_at)
+        return item_chip(s, t)
+
+    a_copies = []
+    for index, (s, t, g) in enumerate(items):
+        chip_at = partner_chip(s, t)
+        if g == 0:
+            weight_rows((chip_at * 2 + 1 - core) * share, share)
+        copy = pair_copy(index, chip_at, g)
+        copy.start()
+        a_copies.append(copy)
+
+    def pair_sum(index, s, t, g):
+        chip_at = item_chip(s, t)
+        a_copies[index].wait_recv()
+        return (
+            part[band(chip_at, core, g)].astype(F32)
+            + recv_a[pl.ds(pl.multiple_of(chip_at * share + g * sub, sub), sub)].astype(F32)
+        )
+
+    b_copies = {}
+    for index, (s, t, g) in enumerate(items):
+        if g == 0:
+            weight_rows((item_chip(s, t) * 2 + core) * share, share)
+        if s == 0:
+            continue
+        at = ((s - 1) * nb + t) * SUBS + g
+        send_b[at] = pair_sum(index, s, t, g).astype(BF16)
+        copy = remote(
+            send_b.at[at],
+            recv_b.at[at],
+            b_s.at[at],
+            b_r.at[at],
+            {"dp": dp_of(lax.rem(a + s, na), b)},
+        )
+        copy.start()
+        b_copies[s, t, g] = copy
+
+    @pl.when(inner)
+    def _():
+        backward_rows(3 * cap, cap)
+        return_copy(3).start()
+        for q in range(slices):
+            near_hop(q).wait_recv()
+            send_d[q] = (held_d[q] + near_d[q].astype(F32)).astype(BF16)
+            far_hop(q).start()
+
+    c_copies = {}
+    for index, (s, t, g) in enumerate(items):
+        if s > 0:
+            continue
+        total = pair_sum(index, s, t, g)
+        for s_from in range(1, na):
+            b_copies[s_from, t, g].wait_recv()
+            total = total + recv_b[((s_from - 1) * nb + t) * SUBS + g].astype(F32)
+        if t > 0:
+            at = (t - 1) * SUBS + g
+            send_c[at] = total.astype(BF16)
+            copy = remote(
+                send_c.at[at],
+                recv_c.at[at],
+                c_s.at[at],
+                c_r.at[at],
+                {"dp": dp_of(a, lax.rem(b + t, nb))},
+            )
+            copy.start()
+            c_copies[t, g] = copy
+        else:
+            w_grad_ref[0, pl.ds(g * sub, sub)] = total
+    for t in range(1, nb):
+        for g in range(SUBS):
+            c_copies[t, g].wait_recv()
+            w_grad_ref[0, pl.ds(g * sub, sub)] += recv_c[(t - 1) * SUBS + g].astype(F32)
+
+    @pl.when(outer)
+    def _():
+        for q in range(slices):
+            far_hop(q).wait_recv()
+            for third in range(3):
+                at = pl.ds(third * hid + q * unit, unit)
+                w_grad_ref[0, :, at] += far_d[q, :, third * unit : (third + 1) * unit].astype(F32)
+
+    return_copy(1).wait_recv()
+    return_copy(2).wait_recv()
+    in_grad_ref[...] = jnp.dot(table_t, arrived[...], preferred_element_type=F32).astype(BF16)
+
+    for args in (x_args, g_args):
+        near_copy(*args).wait_send()
+        cross_copy(*args).wait_send()
+    return_copy(1).wait_send()
+    for j in range(1, n_dp):
+        band_copy(j, *bx_args).wait_send()
+        band_copy(j, *bg_args).wait_send()
+    for q in range(slices):
+        for c in range(4):
+            if c > 0:
+                term_copy(c, q).wait_send()
+            term_over(c, q).wait_send()
+            hand_over(c, q).wait_send()
+        for c in (1, 2):
+            spread(c, q).wait_send()
+        relay(q).wait_send()
+
+    @pl.when(inner)
+    def _():
+        return_copy(2).wait_send()
+        return_copy(3).wait_send()
+        for q in range(slices):
+            weight_on(q).wait_send()
+            far_hop(q).wait_send()
+
+    @pl.when(outer)
+    def _():
+        for q in range(slices):
+            weight_out(q).wait_send()
+            near_hop(q).wait_send()
+
+    for copy in a_copies + list(b_copies.values()) + list(c_copies.values()):
+        copy.wait_send()
+
+
 def local(n_expert, n_dp, tokens, out_grad, gate_prob, routing, expert_weights):
     tok, width = tokens.shape
     full = expert_weights.shape[2]
@@ -368,44 +989,43 @@
     n_b, n_c = max(1, (na - 1) * nb) * SUBS, max(1, nb - 1) * SUBS
     dma = pltpu.SemaphoreType.DMA
     vmem = pl.BlockSpec(memory_space=pltpu.VMEM)
+    weights, rows = pltpu.VMEM((width, full), BF16), pltpu.VMEM((slots, width), BF16)
+    scratch = [weights] + [rows] * 6
+    scratch += [
+        pltpu.VMEM((slots, 2 * hid), BF16),
+        pltpu.VMEM((slots, hid), BF16),
+        pltpu.VMEM((width, full), BF16),
+        pltpu.VMEM((chips * share, full), BF16),
+        pltpu.VMEM((n_b, sub, full), BF16),
+        pltpu.VMEM((n_b, sub, full), BF16),
+        pltpu.VMEM((n_c, sub, full), BF16),
+        pltpu.VMEM((n_c, sub, full), BF16),
+    ]
+    sems = [dma] + [dma((n_expert,))] * 6 + [dma((chips * SUBS,))] * 2
+    sems += [dma((n_b,))] * 2 + [dma((n_c,))] * 2
+    kernel = body
+    if paired(width, hid, n_expert, n_dp):
+        kernel = paired_body
+        slices = hid // 128
+        third = full // slices
+        scratch.insert(1, pltpu.VMEM((slices, width, third), BF16))
+        scratch += [pltpu.VMEM((slices, share, third), BF16)]
+        scratch += [pltpu.VMEM((n_dp * cap, share), BF16)] * 2
+        scratch += [pltpu.VMEM((slices, n_dp * cap, third), BF16)]
+        scratch += [pltpu.VMEM((slices, share, third), F32)]
+        scratch += [pltpu.VMEM((slices, share, third), BF16)] * 3
+        sems.insert(1, dma((slices * 3,)))
+        sems += [dma((n_dp,))] * 4 + [dma((chips * slices,))] * 4 + [dma((slices,))] * 3
+        sems += [dma((chips * slices,))] * 4 + [dma((slices,))] * 3
     early = pl.pallas_call(
-        functools.partial(body, n_expert, n_dp, cap),
+        functools.partial(kernel, n_expert, n_dp, cap),
         out_shape=(
             jax.ShapeDtypeStruct((tok, width), BF16),
             jax.ShapeDtypeStruct((1, share, full), F32),
         ),
         in_specs=[vmem] * 4 + [pl.BlockSpec(memory_space=pl.ANY)],
         out_specs=(vmem, vmem),
-        scratch_shapes=[
-            pltpu.VMEM((width, full), BF16),
-            pltpu.VMEM((slots, width), BF16),
-            pltpu.VMEM((slots, width), BF16),
-            pltpu.VMEM((slots, width), BF16),
-            pltpu.VMEM((slots, width), BF16),
-            pltpu.VMEM((slots, width), BF16),
-            pltpu.VMEM((slots, width), BF16),
-            pltpu.VMEM((slots, 2 * hid), BF16),
-            pltpu.VMEM((slots, hid), BF16),
-            pltpu.VMEM((width, full), BF16),
-            pltpu.VMEM((chips * share, full), BF16),
-            pltpu.VMEM((n_b, sub, full), BF16),
-            pltpu.VMEM((n_b, sub, full), BF16),
-            pltpu.VMEM((n_c, sub, full), BF16),
-            pltpu.VMEM((n_c, sub, full), BF16),
-            dma,
-            dma((n_expert,)),
-            dma((n_expert,)),
-            dma((n_expert,)),
-            dma((n_expert,)),
-            dma((n_expert,)),
-            dma((n_expert,)),
-            dma((chips * SUBS,)),
-            dma((chips * SUBS,)),
-            dma((n_b,)),
-            dma((n_b,)),
-            dma((n_c,)),
-            dma((n_c,)),
-        ],
+        scratch_shapes=scratch + sems,
         compiler_params=pltpu.CompilerParams(
             collective_id=0, has_side_effects=True, vmem_limit_bytes=60 * 1024 * 1024
         ),

time: 85.6 us -> 79.2 us (0.925)
  Pallas kernels: 84.8 us -> 78.4 us
    pallas_call x1, Pallas kernels: 82.5 us -> 76.1 us  [local(): pl.pallas_call(functools.partial(kernel, n_expert, n_dp, cap), out_shape=...]
where the time goes in v2:
time: 79.2 us; the launch traced here: 79.1 us
  Pallas kernels  78.4 us (99%)
    pallas_call x1, Pallas kernels, local(): pl.pallas_call(functools.partial(kernel, n_expert, n_dp, cap), out_shape=...  76.1 us
    pallas_call x1, Pallas kernels, local(): pl.pallas_call(write_out, out_shape=(jax.ShapeDtypeStruct((tok, width), B...  2.32 us

profile of v2, /device:TPU:0, one launch (start us, length us, event | category | flops | bytes accessed | tf_op | source)
XLA Modules:
  0.0 79.1 jit_solution(4159842264018632110)
XLA Ops:
  0.6 76.1 %moe_backward.1 = (bf16[128,2048]{1,0:T(8,128)(2,1)}, f32[1,256,1152]{2,1,0:T(8,128)}) custom-call(bf16[128,2048]{1,0:T(8,128)(2,1)} %tokens_ref.1, bf16[128,2048]{1,0:T(8,128)(2,1)} %out_grad_ref.1, f32[1,128]{1,0:T(1,128)} %bitcast.2, s32[1,128]{1,0:T(1,128)} %bitcast.3, bf16[1,2048,1152]{2,1,0:T(8,128)(2,1)} %w_hbm.1), custom_call_target="tpu_custom_call" | custom-call | tf_op jit(solution)/shard_map/moe_backward/pallas_call | solution.py:1020
  76.7 2.3 %write_out.1 = (bf16[128,2048]{1,0:T(8,128)(2,1)}, f32[1,256,1152]{2,1,0:T(8,128)}) custom-call(bf16[128,2048]{1,0:T(8,128)(2,1)} %get-tuple-element.4.in_grad_ref, f32[1,256,1152]{2,1,0:T(8,128)} %get-tuple-element.5.w_grad_ref), custom_call_target="tpu_custom_call" | custom-call | tf_op jit(solution)/shard_map/write_out/pallas_call | solution.py:1034

commit v3 on v0

--- a/solution.py
+++ b/solution.py
@@ -11,6 +11,7 @@
 F32 = jnp.float32
 BF16 = jnp.bfloat16
 SUBS = 2
+SLICES = 3
 PIECES = 4
 
 
@@ -355,6 +356,626 @@
         copy.wait_send()
 
 
+def paired(width, hid, n_expert, n_dp):
+    chips_a, chips_b = plan(n_expert, n_dp)[3:]
+    return n_expert == 4 and chips_a == chips_b == 2 and width % (128 * n_dp) == hid % (128 * SLICES) == 0
+
+
+def paired_body(
+    n_expert,
+    n_dp,
+    cap,
+    tokens_hbm,
+    out_grad_hbm,
+    gate_hbm,
+    route_hbm,
+    w_hbm,
+    in_grad_ref,
+    w_grad_ref,
+    w_ref,
+    w2_ref,
+    send_x,
+    send_g,
+    recv_x,
+    recv_g,
+    ret,
+    arrived,
+    pair,
+    hidden,
+    part,
+    recv_a,
+    send_b,
+    recv_b,
+    send_c,
+    recv_c,
+    stage,
+    band_x,
+    band_g,
+    terms,
+    held_d,
+    send_d,
+    near_d,
+    far_d,
+    tokens_ref,
+    out_grad_ref,
+    gate_ref,
+    route_ref,
+    w_sem,
+    in_sem,
+    st_sem,
+    to_s,
+    near_r,
+    cross_r,
+    rt_s,
+    rt_r,
+    a_s,
+    a_r,
+    b_s,
+    b_r,
+    c_s,
+    c_r,
+    bd_s,
+    bd_r,
+    tm_s,
+    tm_r,
+    fw_s,
+    fw_r,
+    w_s,
+    w_r,
+    ag_s,
+    ag_r,
+    rl_r,
+    pf_s,
+    pf_r,
+    d_s,
+    d_r,
+):
+    _, _, _, na, nb = plan(n_expert, n_dp)
+    chips = na * nb
+    me = lax.axis_index("expert")
+    dp = lax.axis_index("dp")
+    half = lax.div(me, 2)
+    inner = (me == 1) | (me == n_expert - 2)
+    outer = jnp.logical_not(inner)
+    near = me + 1 - 2 * lax.rem(me, 2)
+    mirror = n_expert - 1 - me
+    inner_far = 2 - half
+    outer_far = 3 - 3 * half
+    tok, width = tokens_hbm.shape
+    hid = w_ref.shape[1] // 3
+    slots = n_expert * cap
+    share = width // n_dp
+    sub = share // SUBS
+    grad_scale = float(tok * n_dp) ** (-0.5)
+    core = lax.rem(dp, 2)
+    chip = lax.div(dp, 2)
+    partner = dp + 1 - 2 * core
+    pos_hi, pos_lo = lax.div(chip, na), lax.rem(chip, na)
+    if na == nb:
+        a = jnp.where(core == 0, pos_lo, pos_hi)
+        b = jnp.where(core == 0, pos_hi, pos_lo)
+    else:
+        a, b = pos_lo, pos_hi
+
+    def chip_of(a_at, b_at):
+        plain = b_at * na + a_at
+        if na == nb:
+            return jnp.where(core == 0, plain, a_at * na + b_at)
+        return plain
+
+    def dp_of(a_at, b_at):
+        return chip_of(a_at, b_at) * 2 + core
+
+    def columns_of(index):
+        return pl.ds(pl.multiple_of(index * share, share), share)
+
+    w_copy = pltpu.make_async_copy(w_hbm.at[0], w_ref, w_sem)
+    slices = w2_ref.shape[0]
+    unit = hid // slices
+
+    def stage_copy(q, third):
+        return pltpu.make_async_copy(
+            w_hbm.at[0, columns_of(dp), pl.ds(third * hid + q * unit, unit)],
+            stage.at[q, :, pl.ds(third * unit, unit)],
+            st_sem.at[q],
+        )
+
+    barrier = pltpu.get_barrier_semaphore()
+    for k in range(1, n_expert):
+        peer = lax.rem(me + k, n_expert)
+        pl.semaphore_signal(barrier, inc=1, device_id={"expert": peer}, device_id_type=MESH)
+    for j in range(1, n_dp):
+        peer = lax.rem(dp + j, n_dp)
+        pl.semaphore_signal(barrier, inc=1, device_id={"dp": peer}, device_id_type=MESH)
+
+    @pl.when(outer)
+    def _():
+        for q in range(slices):
+            for third in range(3):
+                stage_copy(q, third).start()
+
+    loads = [
+        pltpu.make_async_copy(src, dst, in_sem.at[n])
+        for n, (src, dst) in enumerate(
+            (
+                (route_hbm, route_ref),
+                (gate_hbm, gate_ref),
+                (tokens_hbm, tokens_ref),
+                (out_grad_hbm, out_grad_ref),
+            )
+        )
+    ]
+    for load in loads:
+        load.start()
+    w_copy.start()
+
+    def rows_of(index):
+        return pl.ds(index * cap, cap)
+
+    kept = rows_of(3)
+
+    def rows_from(index):
+        return pl.ds(pl.multiple_of(index * cap, cap), cap)
+
+    def remote(src, dst, s_sem, r_sem, device):
+        return pltpu.make_async_remote_copy(
+            src_ref=src,
+            dst_ref=dst,
+            send_sem=s_sem,
+            recv_sem=r_sem,
+            device_id=device,
+            device_id_type=MESH,
+        )
+
+    pl.semaphore_wait(barrier, n_expert - 1 + n_dp - 1)
+
+    def weight_out(q):
+        dst = w2_ref.at[q, columns_of(dp)]
+        return remote(stage.at[q], dst, w_s, w_r.at[q], {"expert": inner_far})
+
+    @pl.when(outer)
+    def _():
+        for q in range(slices):
+            pltpu.make_async_copy(stage.at[q], stage.at[q], st_sem.at[q]).wait()
+            weight_out(q).start()
+
+    row_i = lax.broadcasted_iota(jnp.int32, (tok, tok), 0)
+    col_i = lax.broadcasted_iota(jnp.int32, (tok, tok), 1)
+
+    def column(row):
+        return jnp.sum(jnp.where(row_i == col_i, row, 0.0), axis=1, keepdims=True)
+
+    loads[0].wait()
+    route = route_ref[...]
+    block = jnp.where(route == near, 1, jnp.where(route == inner_far, 2, 3))
+    route_row = jnp.where(route == me, 0, block).astype(F32)
+    route_col = column(route_row)
+    same = route_col == route_row
+    pos_row = jnp.sum(jnp.where(same & (row_i < col_i), 1.0, 0.0), axis=0, keepdims=True)
+    pos_col = jnp.sum(jnp.where(same & (col_i < row_i), 1.0, 0.0), axis=1, keepdims=True)
+    slot_row = route_row * cap + pos_row
+    slot_col = route_col * cap + pos_col
+    slot_at = lax.broadcasted_iota(jnp.int32, (slots, tok), 0).astype(F32)
+    table = jnp.where(slot_at == slot_row, 1.0, 0.0).astype(BF16)
+    slot_of = lax.broadcasted_iota(jnp.int32, (tok, slots), 1).astype(F32)
+    table_t = jnp.where(slot_of == slot_col, 1.0, 0.0).astype(BF16)
+
+    loads[2].wait()
+    send_x[...] = jnp.dot(table, tokens_ref[...], preferred_element_type=F32).astype(BF16)
+    loads[1].wait()
+    loads[3].wait()
+    scaled = (column(gate_ref[...]) * out_grad_ref[...].astype(F32)).astype(BF16)
+    send_g[...] = jnp.dot(table, scaled, preferred_element_type=F32).astype(BF16)
+
+    def run(is_inner):
+        cross_at = 2 if is_inner else 3
+
+        def near_copy(src, dst):
+            return remote(
+                src.at[rows_of(1)], dst.at[rows_of(1)], to_s, near_r, {"expert": near}
+            )
+
+        def cross_copy(src, dst):
+            return remote(
+                src.at[rows_of(2)],
+                dst.at[rows_of(cross_at)],
+                to_s,
+                cross_r.at[cross_at - 2],
+                {"expert": inner_far},
+            )
+
+        def bytes_of(ref, s_sem, r_sem):
+            return remote(ref, ref, s_sem, r_sem, {"expert": near})
+
+        both = pl.ds(0, 2 * cap)
+        x_args = (send_x, recv_x)
+        g_args = (send_g, recv_g)
+
+        def return_copy(index):
+            peer = {1: near, 2: mirror, 3: outer_far}[index]
+            home = rows_of(min(index, 2))
+            return remote(
+                ret.at[rows_of(index)],
+                arrived.at[home],
+                rt_s,
+                rt_r,
+                {"expert": peer},
+            )
+
+        first = jnp.where(core == 0, 1, 2)
+
+        def beside(c):
+            return xor(chip, c)
+
+        chip_first = jnp.where(core == 0, beside(1), beside(2))
+        chip_second = jnp.where(core == 0, beside(2), beside(1))
+
+        def weight_on(q):
+            at = w2_ref.at[q, columns_of(dp)]
+            return remote(at, at, w_s, w_r.at[q], {"expert": near})
+
+        def spread(c, q):
+            at = w2_ref.at[q, columns_of(dp)]
+            return remote(at, at, ag_s, ag_r.at[q], {"dp": beside(c) * 2 + core})
+
+        def relay(q):
+            at = w2_ref.at[q, columns_of(chip_first * 2 + core)]
+            return remote(at, at, ag_s, rl_r.at[q], {"dp": chip_second * 2 + core})
+
+        def hand_over(c, q):
+            at = w2_ref.at[q, columns_of(beside(c) * 2 + core)]
+            return remote(at, at, pf_s, pf_r.at[q], {"dp": partner})
+
+        def band_copy(j, src, dst):
+            peer = lax.rem(dp + j, n_dp)
+            return remote(
+                src.at[kept, columns_of(peer)], dst.at[rows_from(dp)], bd_s, bd_r, {"dp": peer}
+            )
+
+        bands_in = bytes_of(recv_x.at[pl.ds(0, 2 * (n_dp - 1) * cap // n_dp)], bd_s, bd_r)
+
+        def term_copy(c, q):
+            at = terms.at[q, rows_from(dp)]
+            return remote(at, at, tm_s, tm_r.at[q], {"dp": beside(c) * 2 + core})
+
+        def term_over(c, q):
+            at = terms.at[q, rows_from(beside(c) * 2 + core)]
+            return remote(at, at, fw_s, fw_r.at[q], {"dp": partner})
+
+        near_copy(*x_args).start()
+        if not is_inner:
+            near_copy(*g_args).start()
+        cross_copy(*x_args).start()
+        cross_copy(*g_args).start()
+        for j in range(1, n_dp):
+            band_copy(j, send_x, band_x).start()
+            band_copy(j, send_g, band_g).start()
+
+        recv_x[rows_of(0)] = send_x[rows_of(0)]
+        recv_g[rows_of(0)] = send_g[rows_of(0)]
+        band_x[rows_from(dp)] = send_x[kept, columns_of(dp)]
+        band_g[rows_from(dp)] = send_g[kept, columns_of(dp)]
+
+        def forward(x, g, weights):
+            third = weights.shape[1] // 3
+            pre_gate = jnp.dot(x, weights[:, :third], preferred_element_type=F32)
+            pre_up = jnp.dot(x, weights[:, third : 2 * third], preferred_element_type=F32)
+            grad_hidden = jnp.dot(g, weights[:, 2 * third :], preferred_element_type=F32)
+            sig = jax.nn.sigmoid(pre_gate)
+            active = pre_gate * sig
+            grad_gate = grad_hidden * pre_up * (sig * (1.0 + pre_gate * (1.0 - sig)))
+            return (
+                grad_gate.astype(BF16),
+                (grad_hidden * active).astype(BF16),
+                (active * pre_up).astype(BF16),
+            )
+
+        def forward_rows(start, size):
+            rows = pl.ds(start, size)
+            grad_gate, grad_up, kept_hidden = forward(recv_x[rows], recv_g[rows], w_ref)
+            pair[rows, :hid] = grad_gate
+            pair[rows, hid:] = grad_up
+            hidden[rows] = kept_hidden
+
+        def columns(pieces, dst, rows):
+            tile = min(512, width)
+
+            @pl.loop(0, width // tile)
+            def _(j):
+                at = pl.ds(pl.multiple_of(j * tile, tile), tile)
+                total = 0.0
+                for grads, weights in pieces:
+                    total = total + lax.dot_general(
+                        grads(), weights(at), (((1,), (1,)), ((), ())), preferred_element_type=F32
+                    )
+                dst[rows, at] = total.astype(BF16)
+
+        def backward_rows(start, size):
+            rows = pl.ds(start, size)
+            columns([(lambda: pair[rows], lambda at: w_ref[at, : 2 * hid])], ret, rows)
+
+        contract = (((0,), (0,)), ((), ()))
+        mine = rows_from(dp)
+
+        def kept_forward(q):
+            grad_gate, grad_up, kept_hidden = forward(send_x[kept], send_g[kept], w2_ref.at[q])
+            terms[q, mine, :unit] = grad_gate
+            terms[q, mine, unit : 2 * unit] = grad_up
+            terms[q, mine, 2 * unit :] = kept_hidden
+
+        def kept_grad(q):
+            first = lax.dot_general(
+                band_x[...], terms[q, :, : 2 * unit], contract, preferred_element_type=F32
+            )
+            second = lax.dot_general(
+                band_g[...], terms[q, :, 2 * unit :], contract, preferred_element_type=F32
+            )
+            return grad_scale * jnp.concatenate([first, second], axis=1)
+
+        def near_hop(q):
+            return remote(send_d.at[q], near_d.at[q], d_s, d_r.at[q], {"expert": near})
+
+        def far_hop(q):
+            return remote(send_d.at[q], far_d.at[q], d_s, d_r.at[q], {"expert": outer_far})
+
+        def take(q):
+            weight_on(q).wait_recv()
+            if is_inner:
+                weight_on(q).start()
+            for c in (1, 2):
+                spread(c, q).start()
+            hand_over(0, q).start()
+
+        def pass_on(q):
+            bytes_of(w2_ref.at[q, pl.ds(0, 2 * share)], ag_s, ag_r.at[q]).wait_recv()
+            relay(q).start()
+            for c in (1, 2):
+                hand_over(c, q).start()
+
+        def pass_last(q):
+            relay(q).wait_recv()
+            hand_over(3, q).start()
+
+        def kept_terms(q):
+            bytes_of(w2_ref.at[q, pl.ds(0, 4 * share)], pf_s, pf_r.at[q]).wait_recv()
+            kept_forward(q)
+            for c in range(1, 4):
+                term_copy(c, q).start()
+            term_over(0, q).start()
+
+        def pass_terms(q):
+            bytes_of(terms.at[q, pl.ds(0, 3 * cap)], tm_s, tm_r.at[q]).wait_recv()
+            for c in range(1, 4):
+                term_over(c, q).start()
+
+        def kept_band(q):
+            if q == 0:
+                bands_in.wait_recv()
+            bytes_of(terms.at[q, pl.ds(0, 4 * cap)], fw_s, fw_r.at[q]).wait_recv()
+            held_d[q] = kept_grad(q)
+            if not is_inner:
+                send_d[q] = held_d[q].astype(BF16)
+                near_hop(q).start()
+
+        def own_rows():
+            w_copy.wait()
+            forward_rows(0, cap)
+            backward_rows(0, cap)
+            arrived[rows_of(0)] = ret[rows_of(0)]
+
+        def near_forward():
+            bytes_of(recv_x.at[both], to_s, near_r).wait_recv()
+            forward_rows(cap, cap)
+
+        def near_backward():
+            backward_rows(cap, cap)
+            return_copy(1).start()
+
+        def cross_forward(index):
+            bytes_of(recv_x.at[both], to_s, cross_r.at[index - 2]).wait_recv()
+            forward_rows(index * cap, cap)
+
+        def cross_backward(index):
+            backward_rows(index * cap, cap)
+            return_copy(index).start()
+
+        def kept_backward():
+            pieces = [
+                (lambda q=q: terms[q, mine, : 2 * unit], lambda at, q=q: w2_ref[q, at, : 2 * unit])
+                for q in range(slices)
+            ]
+            columns(pieces, arrived, kept)
+
+        def add_hop(q):
+            near_hop(q).wait_recv()
+            send_d[q] = (held_d[q] + near_d[q].astype(F32)).astype(BF16)
+            far_hop(q).start()
+
+        rows_in = slots if is_inner else 2 * cap
+
+        def weight_rows(start, size):
+            at = pl.ds(pl.multiple_of(start, size), size)
+            part[at, : 2 * hid] = (
+                grad_scale
+                * lax.dot_general(
+                    recv_x[:rows_in, at], pair[:rows_in], contract, preferred_element_type=F32
+                )
+            ).astype(BF16)
+            part[at, 2 * hid :] = (
+                grad_scale
+                * lax.dot_general(
+                    recv_g[:rows_in, at], hidden[:rows_in], contract, preferred_element_type=F32
+                )
+            ).astype(BF16)
+
+        def band(chip_at, core_at, g):
+            return pl.ds(pl.multiple_of((chip_at * 2 + core_at) * share + g * sub, sub), sub)
+
+        bands = [(s, t) for s in range(1, na) for t in list(range(1, nb)) + [0]]
+        bands += [(0, t) for t in list(range(1, nb)) + [0]]
+        items = [(s, t, g) for s, t in bands for g in range(SUBS)]
+
+        def item_chip(s, t):
+            return chip_of(lax.rem(a + s, na), lax.rem(b + t, nb))
+
+        def pair_copy(index, chip_at, g):
+            return remote(
+                part.at[band(chip_at, 1 - core, g)],
+                recv_a.at[pl.ds(pl.multiple_of(chip_at * share + g * sub, sub), sub)],
+                a_s,
+                a_r.at[index],
+                {"dp": partner},
+            )
+
+        def partner_chip(s, t):
+            if na == nb:
+                a_at, b_at = lax.rem(b + s, na), lax.rem(a + t, nb)
+                return jnp.where(core == 1, b_at * na + a_at, a_at * na + b_at)
+            return item_chip(s, t)
+
+        def item_pair(index):
+            s, t, g = items[index]
+            return pair_copy(index, partner_chip(s, t), g)
+
+        def item_out(s, t, g):
+            at = ((s - 1) * nb + t) * SUBS + g
+            to = dp_of(lax.rem(a + s, na), b)
+            return remote(send_b.at[at], recv_b.at[at], b_s, b_r.at[at], {"dp": to})
+
+        def item_last(t, g):
+            at = (t - 1) * SUBS + g
+            to = dp_of(a, lax.rem(b + t, nb))
+            return remote(send_c.at[at], recv_c.at[at], c_s, c_r.at[at], {"dp": to})
+
+        def pair_sum(index):
+            s, t, g = items[index]
+            chip_to = item_chip(s, t)
+            item_pair(index).wait_recv()
+            return (
+                part[band(chip_to, core, g)].astype(F32)
+                + recv_a[pl.ds(pl.multiple_of(chip_to * share + g * sub, sub), sub)].astype(F32)
+            )
+
+        def reduce_pair():
+            for index, (s, t, g) in enumerate(items):
+                if g == 0:
+                    weight_rows((partner_chip(s, t) * 2 + 1 - core) * share, share)
+                item_pair(index).start()
+
+        def reduce_first():
+            for index, (s, t, g) in enumerate(items):
+                if g == 0:
+                    weight_rows((item_chip(s, t) * 2 + core) * share, share)
+                if s > 0:
+                    send_b[((s - 1) * nb + t) * SUBS + g] = pair_sum(index).astype(BF16)
+                    item_out(s, t, g).start()
+
+        def item_total(index):
+            s, t, g = items[index]
+            total = pair_sum(index)
+            for s_from in range(1, na):
+                item_out(s_from, t, g).wait_recv()
+                total = total + recv_b[((s_from - 1) * nb + t) * SUBS + g].astype(F32)
+            return total
+
+        def reduce_second():
+            for index, (s, t, g) in enumerate(items):
+                if s == 0 and t > 0:
+                    send_c[(t - 1) * SUBS + g] = item_total(index).astype(BF16)
+                    item_last(t, g).start()
+
+        def reduce_own():
+            for index, (s, t, g) in enumerate(items):
+                if s == t == 0:
+                    w_grad_ref[0, pl.ds(g * sub, sub)] = item_total(index)
+            for t in range(1, nb):
+                for g in range(SUBS):
+                    item_last(t, g).wait_recv()
+                    w_grad_ref[0, pl.ds(g * sub, sub)] += recv_c[(t - 1) * SUBS + g].astype(F32)
+
+        def add_far(q):
+            far_hop(q).wait_recv()
+            for third in range(3):
+                at = pl.ds(third * hid + q * unit, unit)
+                w_grad_ref[0, :, at] += far_d[q, :, third * unit : (third + 1) * unit].astype(F32)
+
+        own_rows()
+        take(0)
+        take(1)
+        pass_on(0)
+        take(2)
+        if is_inner:
+            near_copy(*g_args).start()
+        pass_on(1)
+        pass_last(0)
+        kept_terms(0)
+        pass_on(2)
+        if is_inner:
+            pass_last(1)
+            kept_terms(1)
+            pass_terms(0)
+            pass_last(2)
+            kept_terms(2)
+            near_forward()
+            near_backward()
+            cross_forward(2)
+            cross_backward(2)
+            pass_terms(1)
+            pass_terms(2)
+            cross_forward(3)
+            reduce_pair()
+            reduce_first()
+            kept_band(0)
+            add_hop(0)
+            kept_band(1)
+            add_hop(1)
+            cross_backward(3)
+            reduce_second()
+            kept_band(2)
+            add_hop(2)
+            kept_backward()
+            reduce_own()
+        else:
+            near_forward()
+            pass_last(1)
+            kept_terms(1)
+            pass_terms(0)
+            reduce_pair()
+            kept_band(0)
+            pass_last(2)
+            kept_terms(2)
+            pass_terms(1)
+            kept_band(1)
+            reduce_first()
+            pass_terms(2)
+            kept_band(2)
+            near_backward()
+            kept_backward()
+            reduce_second()
+            reduce_own()
+            for q in range(slices):
+                add_far(q)
+
+        bytes_of(arrived.at[both], rt_s, rt_r).wait_recv()
+        in_grad_ref[...] = jnp.dot(table_t, arrived[...], preferred_element_type=F32).astype(BF16)
+
+        bytes_of(send_x, to_s, near_r).wait_send()
+        bands_in.wait_send()
+        bytes_of(terms.at[:, pl.ds(0, 3 * cap)], tm_s, tm_r.at[0]).wait_send()
+        bytes_of(terms.at[:, pl.ds(0, 4 * cap)], fw_s, fw_r.at[0]).wait_send()
+        bytes_of(w2_ref.at[:, pl.ds(0, 3 * share)], ag_s, ag_r.at[0]).wait_send()
+        bytes_of(w2_ref.at[:, pl.ds(0, 4 * share)], pf_s, pf_r.at[0]).wait_send()
+        bytes_of(stage, w_s, w_r.at[0]).wait_send()
+        bytes_of(send_d, d_s, d_r.at[0]).wait_send()
+        bytes_of(ret.at[pl.ds(0, (3 if is_inner else 1) * cap)], rt_s, rt_r).wait_send()
+        bytes_of(recv_a, a_s, a_r.at[0]).wait_send()
+        bytes_of(send_b, b_s, b_r.at[0]).wait_send()
+        bytes_of(send_c, c_s, c_r.at[0]).wait_send()
+
+    pl.when(inner)(lambda: run(True))
+    pl.when(outer)(lambda: run(False))
+
+
 def local(n_expert, n_dp, tokens, out_grad, gate_prob, routing, expert_weights):
     tok, width = tokens.shape
     full = expert_weights.shape[2]
@@ -368,44 +989,43 @@
     n_b, n_c = max(1, (na - 1) * nb) * SUBS, max(1, nb - 1) * SUBS
     dma = pltpu.SemaphoreType.DMA
     vmem = pl.BlockSpec(memory_space=pltpu.VMEM)
+    weights, rows = pltpu.VMEM((width, full), BF16), pltpu.VMEM((slots, width), BF16)
+    scratch = [weights] + [rows] * 6
+    scratch += [
+        pltpu.VMEM((slots, 2 * hid), BF16),
+        pltpu.VMEM((slots, hid), BF16),
+        pltpu.VMEM((width, full), BF16),
+        pltpu.VMEM((chips * share, full), BF16),
+        pltpu.VMEM((n_b, sub, full), BF16),
+        pltpu.VMEM((n_b, sub, full), BF16),
+        pltpu.VMEM((n_c, sub, full), BF16),
+        pltpu.VMEM((n_c, sub, full), BF16),
+    ]
+    sems = [dma] + [dma((n_expert,))] * 6 + [dma((chips * SUBS,))] * 2
+    sems += [dma((n_b,))] * 2 + [dma((n_c,))] * 2
+    kernel, ins = body, [vmem] * 4
+    if paired(width, hid, n_expert, n_dp):
+        kernel = paired_body
+        slices, third = SLICES, full // SLICES
+        scratch.insert(1, pltpu.VMEM((slices, width, third), BF16))
+        scratch += [pltpu.VMEM((slices, share, third), BF16)]
+        scratch += [pltpu.VMEM((n_dp * cap, share), BF16)] * 2
+        scratch += [pltpu.VMEM((slices, n_dp * cap, third), BF16)]
+        scratch += [pltpu.VMEM((slices, share, third), F32)]
+        scratch += [pltpu.VMEM((slices, share, third), BF16)] * 3
+        scratch += [pltpu.VMEM((tok, width), BF16)] * 2
+        scratch += [pltpu.VMEM((1, tok), F32), pltpu.VMEM((1, tok), jnp.int32)]
+        each = dma((slices,))
+        sems = [dma, dma((4,)), each, dma, dma, dma((2,)), dma, dma]
+        sems += [dma, dma((chips * SUBS,)), dma, dma((n_b,)), dma, dma((n_c,)), dma, dma]
+        sems += [dma, each] * 3 + [dma, each, each] + [dma, each] * 2
+        ins = [pl.BlockSpec(memory_space=pl.ANY)] * 4
     early = pl.pallas_call(
-        functools.partial(body, n_expert, n_dp, cap),
-        out_shape=(
-            jax.ShapeDtypeStruct((tok, width), BF16),
-            jax.ShapeDtypeStruct((1, share, full), F32),
-        ),
-        in_specs=[vmem] * 4 + [pl.BlockSpec(memory_space=pl.ANY)],
+        functools.partial(kernel, n_expert, n_dp, cap),
+        out_shape=(pltpu.VMEM((tok, width), BF16), pltpu.VMEM((1, share, full), F32)),
+        in_specs=ins + [pl.BlockSpec(memory_space=pl.ANY)],
         out_specs=(vmem, vmem),
-        scratch_shapes=[
-            pltpu.VMEM((width, full), BF16),
-            pltpu.VMEM((slots, width), BF16),
-            pltpu.VMEM((slots, width), BF16),
-            pltpu.VMEM((slots, width), BF16),
-            pltpu.VMEM((slots, width), BF16),
-            pltpu.VMEM((slots, width), BF16),
-            pltpu.VMEM((slots, width), BF16),
-            pltpu.VMEM((slots, 2 * hid), BF16),
-            pltpu.VMEM((slots, hid), BF16),
-            pltpu.VMEM((width, full), BF16),
-            pltpu.VMEM((chips * share, full), BF16),
-            pltpu.VMEM((n_b, sub, full), BF16),
-            pltpu.VMEM((n_b, sub, full), BF16),
-            pltpu.VMEM((n_c, sub, full), BF16),
-            pltpu.VMEM((n_c, sub, full), BF16),
-            dma,
-            dma((n_expert,)),
-            dma((n_expert,)),
-            dma((n_expert,)),
-            dma((n_expert,)),
-            dma((n_expert,)),
-            dma((n_expert,)),
-            dma((chips * SUBS,)),
-            dma((chips * SUBS,)),
-            dma((n_b,)),
-            dma((n_b,)),
-            dma((n_c,)),
-            dma((n_c,)),
-        ],
+        scratch_shapes=scratch + sems,
         compiler_params=pltpu.CompilerParams(
             collective_id=0, has_side_effects=True, vmem_limit_bytes=60 * 1024 * 1024
         ),
@@ -417,41 +1037,22 @@
             jax.ShapeDtypeStruct((tok, width), BF16),
             jax.ShapeDtypeStruct((1, share, full), F32),
         ),
-        in_specs=[pl.BlockSpec(memory_space=pl.ANY)] * 2,
+        in_specs=[vmem] * 2,
         out_specs=(pl.BlockSpec(memory_space=pl.ANY),) * 2,
-        scratch_shapes=[
-            pltpu.VMEM((tok, width), BF16),
-            pltpu.VMEM((1, share, full), F32),
-            dma((2 * PIECES,)),
-            dma((2 * PIECES,)),
-        ],
+        scratch_shapes=[dma((2,))],
         name="write_out",
-    )(*early)
-
-
-def write_out(in_grad_ref, w_grad_ref, in_grad_out, w_grad_out, x_held, w_held, in_s, out_s):
-    moves = []
-    for p in range(PIECES):
-        for src, mid, dst in (
-            (in_grad_ref, x_held, in_grad_out),
-            (w_grad_ref.at[0], w_held.at[0], w_grad_out.at[0]),
-        ):
-            rows = src.shape[0] // PIECES
-            at = pl.ds(p * rows, rows)
-            n = len(moves)
-            moves.append(
-                (
-                    pltpu.make_async_copy(src.at[at], mid.at[at], in_s.at[n]),
-                    pltpu.make_async_copy(mid.at[at], dst.at[at], out_s.at[n]),
-                )
-            )
-    for take, _ in moves:
-        take.start()
-    for take, put in moves:
-        take.wait()
-        put.start()
-    for _, put in moves:
-        put.wait()
+    )(*[pltpu.with_memory_space_constraint(value, pltpu.VMEM) for value in early])
+
+
+def write_out(in_grad_ref, w_grad_ref, in_grad_out, w_grad_out, sem):
+    moves = [
+        pltpu.make_async_copy(in_grad_ref, in_grad_out, sem.at[0]),
+        pltpu.make_async_copy(w_grad_ref, w_grad_out, sem.at[1]),
+    ]
+    for move in moves:
+        move.start()
+    for move in moves:
+        move.wait()
 
 
 def solution(mesh):

time: 85.6 us -> 71 us (0.83)
  Pallas kernels: 84.8 us -> 70 us
    pallas_call x1, Pallas kernels: 82.5 us -> 68.8 us  [local(): pl.pallas_call(functools.partial(kernel, n_expert, n_dp, cap), out_shape=...]
    pallas_call x1, Pallas kernels: 2.32 us -> 1.21 us  [local(): pl.pallas_call(write_out, out_shape=(jax.ShapeDtypeStruct((tok, width), B...]
where the time goes in v3:
time: 71 us; the launch traced here: 70.8 us
  Pallas kernels  70 us (99%)
  between operations  0.8 us (1%)
    pallas_call x1, Pallas kernels, local(): pl.pallas_call(functools.partial(kernel, n_expert, n_dp, cap), out_shape=...  68.8 us

profile of v3, /device:TPU:0, one launch (start us, length us, event | category | flops | bytes accessed | tf_op | source)
XLA Modules:
  0.0 70.8 jit_solution(8612951061789621474)
XLA Ops:
  0.6 68.8 %moe_backward.1 = (bf16[128,2048]{1,0:T(8,128)(2,1)S(1)}, f32[1,256,1152]{2,1,0:T(8,128)S(1)}) custom-call(bf16[128,2048]{1,0:T(8,128)(2,1)} %tokens_hbm.1, bf16[128,2048]{1,0:T(8,128)(2,1)} %out_grad_hbm.1, f32[1,128]{1,0:T(1,128)} %bitcast.2, s32[1,128]{1,0:T(1,128)} %bitcast.3, bf16[1,2048,1152]{2,1,0:T(8,128)(2,1)} %w_hbm.1), custom_call_target="tpu_custom_call" | custom-call | tf_op jit(solution)/shard_map/moe_backward/pallas_call | solution.py:1023
  69.5 1.2 %write_out.1 = (bf16[128,2048]{1,0:T(8,128)(2,1)}, f32[1,256,1152]{2,1,0:T(8,128)}) custom-call(bf16[128,2048]{1,0:T(8,128)(2,1)S(1)} %get-tuple-element.4.in_grad_ref, f32[1,256,1152]{2,1,0:T(8,128)S(1)} %get-tuple-element.5.w_grad_ref), custom_call_target="tpu_custom_call" | custom-call | tf_op jit(solution)/shard_map/write_out/pallas_call | solution.py:1034

commit v4 on v3

--- a/solution.py
+++ b/solution.py
@@ -400,6 +400,7 @@
     out_grad_ref,
     gate_ref,
     route_ref,
+    across,
     w_sem,
     in_sem,
     st_sem,
@@ -481,11 +482,15 @@
         )
 
     barrier = pltpu.get_barrier_semaphore()
-    for k in range(1, n_expert):
-        peer = lax.rem(me + k, n_expert)
+    for peer in (near, inner_far):
         pl.semaphore_signal(barrier, inc=1, device_id={"expert": peer}, device_id_type=MESH)
-    for j in range(1, n_dp):
-        peer = lax.rem(dp + j, n_dp)
+
+    @pl.when(inner)
+    def _():
+        pl.semaphore_signal(barrier, inc=1, device_id={"expert": outer_far}, device_id_type=MESH)
+
+    beside_dp = [partner] + [xor(chip, c) * 2 + k for c in (1, 2) for k in (0, 1)]
+    for peer in beside_dp:
         pl.semaphore_signal(barrier, inc=1, device_id={"dp": peer}, device_id_type=MESH)
 
     @pl.when(outer)
@@ -527,7 +532,10 @@
             device_id_type=MESH,
         )
 
-    pl.semaphore_wait(barrier, n_expert - 1 + n_dp - 1)
+    pl.semaphore_wait(barrier, jnp.where(inner, 3, 2) + len(beside_dp))
+    pl.semaphore_signal(
+        across, inc=1, device_id={"dp": xor(chip, 1) * 2 + core}, device_id_type=MESH
+    )
 
     def weight_out(q):
         dst = w2_ref.at[q, columns_of(dp)]
@@ -642,11 +650,14 @@
             at = terms.at[q, rows_from(beside(c) * 2 + core)]
             return remote(at, at, fw_s, fw_r.at[q], {"dp": partner})
 
-        near_copy(*x_args).start()
-        if not is_inner:
-            near_copy(*g_args).start()
+        if is_inner:
+            near_copy(*x_args).start()
         cross_copy(*x_args).start()
         cross_copy(*g_args).start()
+        if not is_inner:
+            near_copy(*x_args).start()
+            near_copy(*g_args).start()
+        pl.semaphore_wait(across, 1)
         for j in range(1, n_dp):
             band_copy(j, send_x, band_x).start()
             band_copy(j, send_g, band_g).start()
@@ -763,21 +774,16 @@
             backward_rows(0, cap)
             arrived[rows_of(0)] = ret[rows_of(0)]
 
-        def near_forward():
+        def near_arrival():
             bytes_of(recv_x.at[both], to_s, near_r).wait_recv()
-            forward_rows(cap, cap)
-
-        def near_backward():
-            backward_rows(cap, cap)
-            return_copy(1).start()
-
-        def cross_forward(index):
+
+        def cross_arrival(index):
             bytes_of(recv_x.at[both], to_s, cross_r.at[index - 2]).wait_recv()
-            forward_rows(index * cap, cap)
-
-        def cross_backward(index):
-            backward_rows(index * cap, cap)
-            return_copy(index).start()
+
+        def return_rows(start, size):
+            backward_rows(start * cap, size * cap)
+            for index in range(start, start + size):
+                return_copy(index).start()
 
         def kept_backward():
             pieces = [
@@ -856,14 +862,19 @@
                 + recv_a[pl.ds(pl.multiple_of(chip_to * share + g * sub, sub), sub)].astype(F32)
             )
 
-        def reduce_pair():
-            for index, (s, t, g) in enumerate(items):
+        sent = [index for index, (s, t, g) in enumerate(items) if s > 0]
+        rest = [index for index, (s, t, g) in enumerate(items) if s == 0]
+
+        def reduce_pair(which):
+            for index in which:
+                s, t, g = items[index]
                 if g == 0:
                     weight_rows((partner_chip(s, t) * 2 + 1 - core) * share, share)
                 item_pair(index).start()
 
-        def reduce_first():
-            for index, (s, t, g) in enumerate(items):
+        def reduce_first(which):
+            for index in which:
+                s, t, g = items[index]
                 if g == 0:
                     weight_rows((item_chip(s, t) * 2 + core) * share, share)
                 if s > 0:
@@ -916,48 +927,54 @@
             pass_terms(0)
             pass_last(2)
             kept_terms(2)
-            near_forward()
-            near_backward()
-            cross_forward(2)
-            cross_backward(2)
+            cross_arrival(3)
+            forward_rows(3 * cap, cap)
+            return_rows(3, 1)
             pass_terms(1)
             pass_terms(2)
-            cross_forward(3)
-            reduce_pair()
-            reduce_first()
             kept_band(0)
+            kept_band(1)
+            near_arrival()
+            cross_arrival(2)
+            forward_rows(cap, 2 * cap)
+            reduce_pair(sent)
+            reduce_first(sent)
             add_hop(0)
-            kept_band(1)
+            return_rows(1, 2)
+            reduce_pair(rest)
+            reduce_first(rest)
             add_hop(1)
-            cross_backward(3)
+            kept_band(2)
             reduce_second()
-            kept_band(2)
             add_hop(2)
             kept_backward()
             reduce_own()
         else:
-            near_forward()
+            near_arrival()
+            forward_rows(cap, cap)
             pass_last(1)
+            pass_terms(0)
             kept_terms(1)
-            pass_terms(0)
-            reduce_pair()
             kept_band(0)
             pass_last(2)
+            reduce_pair(sent + rest)
             kept_terms(2)
             pass_terms(1)
             kept_band(1)
-            reduce_first()
+            reduce_first(sent + rest)
             pass_terms(2)
             kept_band(2)
-            near_backward()
+            return_rows(1, 1)
             kept_backward()
             reduce_second()
             reduce_own()
-            for q in range(slices):
+            for q in range(slices - 1):
                 add_far(q)
 
         bytes_of(arrived.at[both], rt_s, rt_r).wait_recv()
         in_grad_ref[...] = jnp.dot(table_t, arrived[...], preferred_element_type=F32).astype(BF16)
+        if not is_inner:
+            add_far(slices - 1)
 
         bytes_of(send_x, to_s, near_r).wait_send()
         bands_in.wait_send()
@@ -1016,7 +1033,7 @@
         scratch += [pltpu.VMEM((tok, width), BF16)] * 2
         scratch += [pltpu.VMEM((1, tok), F32), pltpu.VMEM((1, tok), jnp.int32)]
         each = dma((slices,))
-        sems = [dma, dma((4,)), each, dma, dma, dma((2,)), dma, dma]
+        sems = [pltpu.SemaphoreType.REGULAR, dma, dma((4,)), each, dma, dma, dma((2,)), dma, dma]
         sems += [dma, dma((chips * SUBS,)), dma, dma((n_b,)), dma, dma((n_c,)), dma, dma]
         sems += [dma, each] * 3 + [dma, each, each] + [dma, each] * 2
         ins = [pl.BlockSpec(memory_space=pl.ANY)] * 4

time: 71 us -> 70.5 us (level)
  no operation moved by 1% of the time
where the time goes in v4:
time: 70.5 us; the launch traced here: 70.3 us
  Pallas kernels  69.5 us (99%)
  between operations  0.8 us (1%)
    pallas_call x1, Pallas kernels, local(): pl.pallas_call(functools.partial(kernel, n_expert, n_dp, cap), out_shape=...  68.3 us

profile of v4, /device:TPU:0, one launch (start us, length us, event | category | flops | bytes accessed | tf_op | source)
XLA Modules:
  0.0 70.3 jit_solution(11147353108942765315)
XLA Ops:
  0.6 68.3 %moe_backward.1 = (bf16[128,2048]{1,0:T(8,128)(2,1)S(1)}, f32[1,256,1152]{2,1,0:T(8,128)S(1)}) custom-call(bf16[128,2048]{1,0:T(8,128)(2,1)} %tokens_hbm.1, bf16[128,2048]{1,0:T(8,128)(2,1)} %out_grad_hbm.1, f32[1,128]{1,0:T(1,128)} %bitcast.2, s32[1,128]{1,0:T(1,128)} %bitcast.3, bf16[1,2048,1152]{2,1,0:T(8,128)(2,1)} %w_hbm.1), custom_call_target="tpu_custom_call" | custom-call | tf_op jit(solution)/shard_map/moe_backward/pallas_call | solution.py:1040
  69.0 1.2 %write_out.1 = (bf16[128,2048]{1,0:T(8,128)(2,1)}, f32[1,256,1152]{2,1,0:T(8,128)}) custom-call(bf16[128,2048]{1,0:T(8,128)(2,1)S(1)} %get-tuple-element.4.in_grad_ref, f32[1,256,1152]{2,1,0:T(8,128)S(1)} %get-tuple-element.5.w_grad_ref), custom_call_target="tpu_custom_call" | custom-call | tf_op jit(solution)/shard_map/write_out/pallas_call | solution.py:1051

commit v5 on v4

--- a/solution.py
+++ b/solution.py
@@ -780,11 +780,6 @@
         def cross_arrival(index):
             bytes_of(recv_x.at[both], to_s, cross_r.at[index - 2]).wait_recv()
 
-        def return_rows(start, size):
-            backward_rows(start * cap, size * cap)
-            for index in range(start, start + size):
-                return_copy(index).start()
-
         def kept_backward():
             pieces = [
                 (lambda q=q: terms[q, mine, : 2 * unit], lambda at, q=q: w2_ref[q, at, : 2 * unit])
@@ -929,7 +924,8 @@
             kept_terms(2)
             cross_arrival(3)
             forward_rows(3 * cap, cap)
-            return_rows(3, 1)
+            backward_rows(3 * cap, cap)
+            return_copy(3).start()
             pass_terms(1)
             pass_terms(2)
             kept_band(0)
@@ -938,15 +934,18 @@
             cross_arrival(2)
             forward_rows(cap, 2 * cap)
             reduce_pair(sent)
+            backward_rows(cap, cap)
+            return_copy(1).start()
             reduce_first(sent)
             add_hop(0)
-            return_rows(1, 2)
+            backward_rows(2 * cap, cap)
             reduce_pair(rest)
             reduce_first(rest)
             add_hop(1)
             kept_band(2)
             reduce_second()
             add_hop(2)
+            return_copy(2).start()
             kept_backward()
             reduce_own()
         else:
@@ -957,14 +956,17 @@
             kept_terms(1)
             kept_band(0)
             pass_last(2)
-            reduce_pair(sent + rest)
+            reduce_pair(sent)
             kept_terms(2)
+            reduce_first(sent)
             pass_terms(1)
+            reduce_pair(rest)
+            reduce_first(rest)
             kept_band(1)
-            reduce_first(sent + rest)
             pass_terms(2)
             kept_band(2)
-            return_rows(1, 1)
+            backward_rows(cap, cap)
+            return_copy(1).start()
             kept_backward()
             reduce_second()
             reduce_own()

time: 70.5 us -> 69.7 us (0.989)
    pallas_call x1, Pallas kernels: 68.3 us -> 67.6 us  [local(): pl.pallas_call(functools.partial(kernel, n_expert, n_dp, cap), out_shape=...]
where the time goes in v5:
time: 69.7 us; the launch traced here: 69.6 us
  Pallas kernels  68.8 us (99%)
  between operations  0.8 us (1%)
    pallas_call x1, Pallas kernels, local(): pl.pallas_call(functools.partial(kernel, n_expert, n_dp, cap), out_shape=...  67.6 us

profile of v5, /device:TPU:0, one launch (start us, length us, event | category | flops | bytes accessed | tf_op | source)
XLA Modules:
  0.0 69.6 jit_solution(16769010281368062056)
XLA Ops:
  0.6 67.6 %moe_backward.1 = (bf16[128,2048]{1,0:T(8,128)(2,1)S(1)}, f32[1,256,1152]{2,1,0:T(8,128)S(1)}) custom-call(bf16[128,2048]{1,0:T(8,128)(2,1)} %tokens_hbm.1, bf16[128,2048]{1,0:T(8,128)(2,1)} %out_grad_hbm.1, f32[1,128]{1,0:T(1,128)} %bitcast.2, s32[1,128]{1,0:T(1,128)} %bitcast.3, bf16[1,2048,1152]{2,1,0:T(8,128)(2,1)} %w_hbm.1), custom_call_target="tpu_custom_call" | custom-call | tf_op jit(solution)/shard_map/moe_backward/pallas_call | solution.py:1042
  68.2 1.2 %write_out.1 = (bf16[128,2048]{1,0:T(8,128)(2,1)}, f32[1,256,1152]{2,1,0:T(8,128)}) custom-call(bf16[128,2048]{1,0:T(8,128)(2,1)S(1)} %get-tuple-element.4.in_grad_ref, f32[1,256,1152]{2,1,0:T(8,128)S(1)} %get-tuple-element.5.w_grad_ref), custom_call_target="tpu_custom_call" | custom-call | tf_op jit(solution)/shard_map/write_out/pallas_call | solution.py:1053

commit v6 on v5

--- a/solution.py
+++ b/solution.py
@@ -565,8 +565,6 @@
     slot_col = route_col * cap + pos_col
     slot_at = lax.broadcasted_iota(jnp.int32, (slots, tok), 0).astype(F32)
     table = jnp.where(slot_at == slot_row, 1.0, 0.0).astype(BF16)
-    slot_of = lax.broadcasted_iota(jnp.int32, (tok, slots), 1).astype(F32)
-    table_t = jnp.where(slot_of == slot_col, 1.0, 0.0).astype(BF16)
 
     loads[2].wait()
     send_x[...] = jnp.dot(table, tokens_ref[...], preferred_element_type=F32).astype(BF16)
@@ -606,7 +604,7 @@
                 ret.at[rows_of(index)],
                 arrived.at[home],
                 rt_s,
-                rt_r,
+                rt_r.at[min(index, 2) - 1],
                 {"expert": peer},
             )
 
@@ -779,6 +777,23 @@
 
         def cross_arrival(index):
             bytes_of(recv_x.at[both], to_s, cross_r.at[index - 2]).wait_recv()
+
+        def home_rows(start, size):
+            at = lax.broadcasted_iota(jnp.int32, (tok, size * cap), 1).astype(F32) + start * cap
+            pick = jnp.where(at == slot_col, 1.0, 0.0).astype(BF16)
+            rows = arrived[start * cap : (start + size) * cap]
+            return jnp.dot(pick, rows, preferred_element_type=F32).astype(BF16)
+
+        def await_home(index):
+            bytes_of(arrived.at[rows_of(index)], rt_s, rt_r.at[index - 1]).wait_recv()
+
+        def home_early():
+            if is_inner:
+                await_home(1)
+                in_grad_ref[...] = home_rows(0, 2) + home_rows(3, 1)
+            else:
+                await_home(2)
+                in_grad_ref[...] = home_rows(0, 1) + home_rows(2, 2)
 
         def kept_backward():
             pieces = [
@@ -947,6 +962,7 @@
             add_hop(2)
             return_copy(2).start()
             kept_backward()
+            home_early()
             reduce_own()
         else:
             near_arrival()
@@ -969,14 +985,14 @@
             return_copy(1).start()
             kept_backward()
             reduce_second()
+            home_early()
             reduce_own()
-            for q in range(slices - 1):
+            for q in range(slices):
                 add_far(q)
 
-        bytes_of(arrived.at[both], rt_s, rt_r).wait_recv()
-        in_grad_ref[...] = jnp.dot(table_t, arrived[...], preferred_element_type=F32).astype(BF16)
-        if not is_inner:
-            add_far(slices - 1)
+        late = 2 if is_inner else 1
+        await_home(late)
+        in_grad_ref[...] += home_rows(late, 1)
 
         bytes_of(send_x, to_s, near_r).wait_send()
         bands_in.wait_send()
@@ -986,7 +1002,7 @@
         bytes_of(w2_ref.at[:, pl.ds(0, 4 * share)], pf_s, pf_r.at[0]).wait_send()
         bytes_of(stage, w_s, w_r.at[0]).wait_send()
         bytes_of(send_d, d_s, d_r.at[0]).wait_send()
-        bytes_of(ret.at[pl.ds(0, (3 if is_inner else 1) * cap)], rt_s, rt_r).wait_send()
+        bytes_of(ret.at[pl.ds(0, (3 if is_inner else 1) * cap)], rt_s, rt_r.at[0]).wait_send()
         bytes_of(recv_a, a_s, a_r.at[0]).wait_send()
         bytes_of(send_b, b_s, b_r.at[0]).wait_send()
         bytes_of(send_c, c_s, c_r.at[0]).wait_send()
@@ -1035,7 +1051,8 @@
         scratch += [pltpu.VMEM((tok, width), BF16)] * 2
         scratch += [pltpu.VMEM((1, tok), F32), pltpu.VMEM((1, tok), jnp.int32)]
         each = dma((slices,))
-        sems = [pltpu.SemaphoreType.REGULAR, dma, dma((4,)), each, dma, dma, dma((2,)), dma, dma]
+        sems = [pltpu.SemaphoreType.REGULAR, dma, dma((4,)), each, dma, dma]
+        sems += [dma((2,)), dma, dma((2,))]
         sems += [dma, dma((chips * SUBS,)), dma, dma((n_b,)), dma, dma((n_c,)), dma, dma]
         sems += [dma, each] * 3 + [dma, each, each] + [dma, each] * 2
         ins = [pl.BlockSpec(memory_space=pl.ANY)] * 4

time: 69.7 us -> 69.6 us (level)
  no operation moved by 1% of the time
where the time goes in v6:
time: 69.6 us; the launch traced here: 69.5 us
  Pallas kernels  68.7 us (99%)
  between operations  0.8 us (1%)
    pallas_call x1, Pallas kernels, local(): pl.pallas_call(functools.partial(kernel, n_expert, n_dp, cap), out_shape=...  67.5 us

profile of v6, /device:TPU:0, one launch (start us, length us, event | category | flops | bytes accessed | tf_op | source)
XLA Modules:
  0.0 69.5 jit_solution(2592471527713556339)
XLA Ops:
  0.6 67.5 %moe_backward.1 = (bf16[128,2048]{1,0:T(8,128)(2,1)S(1)}, f32[1,256,1152]{2,1,0:T(8,128)S(1)}) custom-call(bf16[128,2048]{1,0:T(8,128)(2,1)} %tokens_hbm.1, bf16[128,2048]{1,0:T(8,128)(2,1)} %out_grad_hbm.1, f32[1,128]{1,0:T(1,128)} %bitcast.2, s32[1,128]{1,0:T(1,128)} %bitcast.3, bf16[1,2048,1152]{2,1,0:T(8,128)(2,1)} %w_hbm.1), custom_call_target="tpu_custom_call" | custom-call | tf_op jit(solution)/shard_map/moe_backward/pallas_call | solution.py:1059
  68.1 1.2 %write_out.1 = (bf16[128,2048]{1,0:T(8,128)(2,1)}, f32[1,256,1152]{2,1,0:T(8,128)}) custom-call(bf16[128,2048]{1,0:T(8,128)(2,1)S(1)} %get-tuple-element.4.in_grad_ref, f32[1,256,1152]{2,1,0:T(8,128)S(1)} %get-tuple-element.5.w_grad_ref), custom_call_target="tpu_custom_call" | custom-call | tf_op jit(solution)/shard_map/write_out/pallas_call | solution.py:1070
